TPU v7x, 128 devices: a whole 4x4x4 slice. The times are simulated.
128 devices in a mesh: ctx: 16 (over y, x), tp: 8 (over z, core).
Axes of the slice: x: 4, y: 4, z: 4, core: 2. Of those that a mesh axis runs over, the one named last changes fastest.
Arguments:
- tokens: bfloat16 [8192, 4096], P('ctx'), may hold values from -48 to 48
- w_query: bfloat16 [4096, 4096], P(None, 'tp'), may hold values from -0.09375 to 0.09375
- w_key: bfloat16 [4096, 4096], P(None, 'tp'), may hold values from -0.09375 to 0.09375
- w_value: bfloat16 [4096, 4096], P(None, 'tp'), may hold values from -0.09375 to 0.09375
- w_out: bfloat16 [4096, 4096], P('tp'), may hold values from -0.09375 to 0.09375
- block_doc: int32 [128], replicated, may hold values from 0 to 1, never falling along the last dimension, each value on 1 to 112 neighbouring positions
- grad_out: bfloat16 [8192, 4096], P('ctx', 'tp'), may hold values from -6 to 6
Outputs:
- output: bfloat16 [8192, 4096], P('ctx', 'tp')
- grad_tokens: bfloat16 [8192, 4096], P('ctx', 'tp')
- grad_query_weight: float32 [4096, 4096], P('ctx', 'tp')
- grad_key_weight: float32 [4096, 4096], P('ctx', 'tp')
- grad_value_weight: float32 [4096, 4096], P('ctx', 'tp')
- grad_out_weight: float32 [4096, 4096], P('tp', 'ctx')
Inputs may be any that keep to these rules, and one draw needn't show every extreme that they name: block_doc never falls along the blocks; each document covers 1 to 112 consecutive blocks.
All inputs are finite; a program needn't handle non-finite values.
Results may differ from a plain program's by a relative error of at most 0.024.
The roundings to bfloat16 on the way count: a program that leaves them out, or rounds other values in their place, can miss the bound.
Values may be sent and summed in bfloat16 or wider, within the bound.
A program may use at most 192 MiB of HBM per device.

v0:
```python
import math

import jax
import jax.numpy as jnp
from jax import lax
from jax.sharding import PartitionSpec as P

HDIM = 128
BLOCK = 64


big_negative = -1e30


def cut_along(shard, dim, length):
    dims = shard.shape
    blocks = shard.reshape(*dims[:dim], length, dims[dim] // length, *dims[dim + 1 :])
    return jnp.moveaxis(blocks, dim, 0)


def summed_on_arrival(shard, axis, dim):
    length = lax.axis_size(axis)
    blocks = lax.all_to_all(cut_along(shard, dim, length), axis, 0, 0, tiled=True)
    return jnp.sum(blocks, axis=0)


def in_one_piece(arrays, axis, dim, along):
    widths = [a.shape[along] for a in arrays]
    both = jnp.concatenate(arrays, axis=along)
    out = summed_on_arrival(both, axis, dim)
    return tuple(jnp.split(out, [sum(widths[:k]) for k in range(1, len(widths))], axis=along))


def sent_and_summed(shard, axis, dim):
    length = lax.axis_size(axis)
    blocks = lax.all_to_all(cut_along(shard, dim, length), axis, 0, 0, tiled=True)
    return jnp.sum(blocks.astype(jnp.float32), axis=0)


def elementwise_product(pattern, left_side, right_side):
    return jnp.einsum(pattern, left_side, right_side, preferred_element_type=jnp.float32)


def attend(
    query_row_matrix,
    key_row_matrix,
    value_row_matrix,
    summary_key,
    summary_value,
    allowed,
    causal,
    score_scale_factor,
):
    near_scores = (
        elementwise_product("nqhd,nkhd->nhqk", query_row_matrix, key_row_matrix)
        * score_scale_factor
    )
    near_scores = jnp.where(causal[None, None], near_scores, big_negative)
    distant_score_matrix = (
        elementwise_product("yzxo,lxo->yzxl", query_row_matrix, summary_key) * score_scale_factor
    )
    distant_score_matrix = jnp.where(allowed[:, None, None, :], distant_score_matrix, big_negative)
    row_top = jnp.maximum(
        jnp.transpose(jnp.max(near_scores, axis=3), (0, 2, 1)),
        jnp.max(distant_score_matrix, axis=3),
    )
    near_exp = jnp.exp(near_scores - jnp.transpose(row_top, (0, 2, 1))[..., None])
    far_exp = jnp.exp(distant_score_matrix - row_top[..., None])
    denom_sum = jnp.transpose(jnp.sum(near_exp, axis=3), (0, 2, 1)) + jnp.sum(far_exp, axis=3)
    local_weight = (near_exp / jnp.transpose(denom_sum, (0, 2, 1))[..., None]).astype(jnp.bfloat16)
    distant_weight = (far_exp / denom_sum[..., None]).astype(jnp.bfloat16)
    combined_output = elementwise_product(
        "jvyb,jbvo->jyvo", local_weight, value_row_matrix
    ) + elementwise_product("gtuv,vuk->gtuk", distant_weight, summary_value)
    return (combined_output.astype(jnp.bfloat16), local_weight, distant_weight)


def attend_back(
    query_row_matrix,
    key_row_matrix,
    value_row_matrix,
    summary_key,
    summary_value,
    combined_output,
    local_weight,
    distant_weight,
    incoming_gradient,
    score_scale_factor,
):
    row_delta = jnp.sum(
        combined_output.astype(jnp.float32) * incoming_gradient.astype(jnp.float32), axis=3
    )
    near_d = elementwise_product("nqhd,nkhd->nhqk", incoming_gradient, value_row_matrix)
    distant_gradient_term = elementwise_product("yzxo,lxo->yzxl", incoming_gradient, summary_value)
    local_score_sum = (
        local_weight.astype(jnp.float32) * (near_d - jnp.transpose(row_delta, (0, 2, 1))[..., None])
    ).astype(jnp.bfloat16)
    distant_score_sum = (
        distant_weight.astype(jnp.float32) * (distant_gradient_term - row_delta[..., None])
    ).astype(jnp.bfloat16)
    query_gradient = (
        elementwise_product("jvyb,jbvo->jyvo", local_score_sum, key_row_matrix)
        + elementwise_product("gtuv,vuk->gtuk", distant_score_sum, summary_key)
    ) * score_scale_factor
    d_key = (
        elementwise_product("nhqk,nqhd->nkhd", local_score_sum, query_row_matrix)
        * score_scale_factor
    )
    d_value = elementwise_product("nhqk,nqhd->nkhd", local_weight, incoming_gradient)
    summary_key_gradient = (
        elementwise_product("agwi,agwu->iwu", distant_score_sum, query_row_matrix)
        * score_scale_factor
    )
    summary_value_gradient = elementwise_product(
        "agwi,agwu->iwu", distant_weight, incoming_gradient
    )
    return (query_gradient, d_key, d_value, summary_key_gradient, summary_value_gradient)


def back_project(grad_rows, weight):
    return lax.dot_general(
        grad_rows, weight, (((1,), (1,)), ((), ())), preferred_element_type=jnp.float32
    )


def term_maker(tokens, grad_rows):
    return lax.dot_general(
        tokens, grad_rows, (((0,), (0,)), ((), ())), preferred_element_type=jnp.float32
    )


def per_device(tokens, w_query, w_key, w_value, w_out, block_doc, grad_out):
    score_scale_factor = 1.0 / math.sqrt(HDIM)
    tok_rows = tokens.shape[0]
    col_count = w_query.shape[1]
    blocks = tok_rows // BLOCK
    head_count = col_count // HDIM
    block_shape = (blocks, BLOCK, head_count, HDIM)

    def project(weight):
        return jnp.dot(tokens, weight, preferred_element_type=jnp.float32).astype(jnp.bfloat16)

    query_row_matrix = project(w_query).reshape(block_shape)
    key_row_matrix = project(w_key).reshape(block_shape)
    value_row_matrix = project(w_value).reshape(block_shape)
    own_key = key_row_matrix[:, BLOCK - 1].reshape(blocks, col_count)
    own_value = value_row_matrix[:, BLOCK - 1].reshape(blocks, col_count)
    summary_key, summary_value = (
        lax.all_gather(own_key, "ctx", axis=0, tiled=True),
        lax.all_gather(own_value, "ctx", axis=0, tiled=True),
    )
    total_blocks = summary_key.shape[0]
    summary_key = summary_key.reshape(total_blocks, head_count, HDIM)
    summary_value = summary_value.reshape(total_blocks, head_count, HDIM)
    first_block = lax.axis_index("ctx") * blocks
    query_ids = first_block + jnp.arange(blocks, dtype=jnp.int32)
    own_doc = lax.dynamic_slice_in_dim(block_doc, first_block, blocks, 0)
    block_ids = jnp.arange(total_blocks, dtype=jnp.int32)
    allowed = (block_ids[None, :] < query_ids[:, None]) & (block_doc[None, :] == own_doc[:, None])
    positions = jnp.arange(BLOCK, dtype=jnp.int32)
    causal = positions[None, :] <= positions[:, None]
    combined_output, local_weight, distant_weight = attend(
        query_row_matrix,
        key_row_matrix,
        value_row_matrix,
        summary_key,
        summary_value,
        allowed,
        causal,
        score_scale_factor,
    )
    attn = combined_output.reshape(tok_rows, col_count)
    partial_value = jnp.dot(attn, w_out, preferred_element_type=jnp.float32)
    summed = lax.psum_scatter(partial_value, "tp", scatter_dimension=1, tiled=True)
    shard_width = summed.shape[1]
    residual = lax.dynamic_slice_in_dim(tokens, lax.axis_index("tp") * shard_width, shard_width, 1)
    output = (residual.astype(jnp.float32) + summed).astype(jnp.bfloat16)
    upstream_full = lax.all_gather(grad_out, "tp", axis=1, tiled=True)
    d_attn = back_project(upstream_full, w_out).astype(jnp.bfloat16)
    grads = attend_back(
        query_row_matrix,
        key_row_matrix,
        value_row_matrix,
        summary_key,
        summary_value,
        combined_output,
        local_weight,
        distant_weight,
        d_attn.reshape(block_shape),
        score_scale_factor,
    )
    query_gradient, d_key, d_value, summary_key_gradient, summary_value_gradient = grads
    flat_key = summary_key_gradient.reshape(total_blocks, col_count)
    flat_value = summary_value_gradient.reshape(total_blocks, col_count)
    back_key, back_value = in_one_piece((flat_key, flat_value), "ctx", 0, 1)
    query_gradient = query_gradient.astype(jnp.bfloat16).reshape(tok_rows, col_count)
    d_key = (
        d_key.at[:, BLOCK - 1]
        .add(back_key.reshape(blocks, head_count, HDIM))
        .astype(jnp.bfloat16)
        .reshape(tok_rows, col_count)
    )
    d_value = (
        d_value.at[:, BLOCK - 1]
        .add(back_value.reshape(blocks, head_count, HDIM))
        .astype(jnp.bfloat16)
        .reshape(tok_rows, col_count)
    )
    d_partial = (
        back_project(query_gradient, w_query)
        + back_project(d_key, w_key)
        + back_project(d_value, w_value)
    )
    d_summed = lax.psum_scatter(d_partial, "tp", scatter_dimension=1, tiled=True)
    grad_tokens = (grad_out.astype(jnp.float32) + d_summed).astype(jnp.bfloat16)
    stacked = jnp.concatenate([query_gradient, d_key, d_value], axis=1)
    joined = lax.psum_scatter(
        term_maker(tokens, stacked).astype(jnp.bfloat16), "ctx", scatter_dimension=0, tiled=True
    ).astype(jnp.float32)
    grad_query_weight = joined[:, :col_count]
    grad_key_weight = joined[:, col_count : 2 * col_count]
    grad_value_weight = joined[:, 2 * col_count :]
    out_term = lax.dot_general(
        attn, upstream_full, (((0,), (0,)), ((), ())), preferred_element_type=jnp.float32
    )
    grad_out_weight = sent_and_summed(out_term.astype(jnp.bfloat16), "ctx", 1)
    return (
        output,
        grad_tokens,
        grad_query_weight,
        grad_key_weight,
        grad_value_weight,
        grad_out_weight,
    )


def solution(mesh):
    in_specs = (
        P("ctx", None),
        P(None, "tp"),
        P(None, "tp"),
        P(None, "tp"),
        P("tp", None),
        P(),
        P("ctx", "tp"),
    )
    out_specs = (
        P("ctx", "tp"),
        P("ctx", "tp"),
        P("ctx", "tp"),
        P("ctx", "tp"),
        P("ctx", "tp"),
        P("tp", "ctx"),
    )
    return jax.shard_map(
        per_device, mesh=mesh, in_specs=in_specs, out_specs=out_specs, check_vma=False
    )
```

profile of v0, /device:TPU:1, one launch (start us, length us, event | category | flops | bytes accessed | tf_op | source)
XLA Modules:
  0.0 308.5 jit_solution(12927653725125463821)
XLA Ops:
  7.2 0.7 all-gather.2.cloned.1.call-update
  8.0 5.8 %convolution_convert_fusion.4 = bf16[512,512]{1,0:T(8,128)(2,1)S(1)} fusion(bf16[512,4096]{1,0:T(8,128)(2,1)} %param.11, bf16[4096,512]{1,0:T(8,128)(2,1)} %param.12), kind=kOutput, calls=%fused_computation.28 | convolution fusion | flops 2147745792 | bytes 8912896 | tf_op jit(solution)/shard_map/dot_general | solution.py:141
  14.0 5.8 %convolution_convert_fusion.3 = bf16[512,512]{1,0:T(8,128)(2,1)S(1)} fusion(bf16[512,4096]{1,0:T(8,128)(2,1)} %param.11, bf16[4096,512]{1,0:T(8,128)(2,1)} %param.13), kind=kOutput, calls=%fused_computation.27 | convolution fusion | flops 2147745792 | bytes 8912896 | tf_op jit(solution)/shard_map/dot_general | solution.py:141
  20.0 21.5 %all_gather.9 = bf16[128,512]{1,0:T(8,128)(2,1)S(1)} all-gather(bf16[8,512]{1,0:T(8,128)(2,1)S(1)} %bitcast.180), channel_id=1, replica_groups=mesh['ctx'=16,'tp'=8] {'ctx'}, dimensions={0}, use_global_device_ids=true | all-gather | bytes 139264 | tf_op jit(solution)/shard_map/all_gather | solution.py:149
  41.6 5.9 %convolution_convert_fusion.5 = bf16[512,512]{1,0:T(8,128)(2,1)S(1)} fusion(bf16[512,4096]{1,0:T(8,128)(2,1)} %param.11, bf16[4096,512]{1,0:T(8,128)(2,1)} %param.14), kind=kOutput, calls=%fused_computation.29 | convolution fusion | flops 2147745792 | bytes 8912896 | tf_op jit(solution)/shard_map/dot_general | solution.py:141
  47.7 17.8 %all_gather.10 = bf16[128,512]{1,0:T(8,128)(2,1)S(1)} all-gather(bf16[8,512]{1,0:T(8,128)(2,1)S(1)} %bitcast.181), channel_id=1, replica_groups=mesh['ctx'=16,'tp'=8] {'ctx'}, dimensions={0}, use_global_device_ids=true | all-gather | bytes 139264 | tf_op jit(solution)/shard_map/all_gather | solution.py:150
  66.4 0.4 fusion.44
  67.1 0.6 fusion.18
  68.0 1.3 convolution_bitcast_fusion.3
  69.4 5.8 %convolution_convert_fusion.2 = bf16[512,512]{1,0:T(8,128)(2,1)S(1)} fusion(bf16[512,4096]{1,0:T(8,128)(2,1)} %all-gather.2.cloned.1.call-done, bf16[512,4096]{1,0:T(8,128)(2,1)} %param.15), kind=kOutput, calls=%fused_computation.26 | convolution fusion | flops 2147745792 | bytes 8912896 | tf_op jit(solution)/shard_map/dot_general | solution.py:121
  75.4 3.0 multiply_reduce_fusion
  78.8 5.6 %fusion.21 = f32[512,4096]{1,0:T(8,128)} fusion(bf16[512,4096]{1,0:T(8,128)(2,1)S(1)} %copy-done.7, bf16[64,8,4,128]{3,2,1,0:T(4,128)(2,1)S(1)} %bitcast.163), kind=kOutput, calls=%fused_computation.51 | convolution fusion | flops 2147483648 | bytes 13107200 | tf_op jit(solution)/shard_map/dot_general | solution.py:173
  84.4 0.9 copy.174
  85.3 1.8 convolution_bitcast_fusion.4
  87.2 1.1 copy.183
  88.3 0.8 concatenate.16
  89.4 1.1 copy-done.4
  90.4 0.6 slice.79
  91.1 0.7 copy.175
  91.8 1.3 fusion.46
  93.1 1.7 multiply_convert_fusion
  94.9 0.8 copy-done.12
  95.7 1.1 fusion.16
  96.7 1.2 copy.181
  97.9 0.8 concatenate.15
  98.7 1.9 pad_maximum_fusion
  100.6 4.3 %all-to-all-start = ((f32[16,8,1024]{2,1,0:T(8,128)}), f32[16,8,1024]{2,1,0:T(8,128)}, u32[]{:S(2)}, u32[]{:S(2)}) async-start(f32[16,8,1024]{2,1,0:T(8,128)} %pad_maximum_fusion), calls=%async_computation.1 | async-start | bytes 1048576 | tf_op jit(solution)/shard_map/all_to_all | solution.py:23
  105.1 1.4 fusion.12
  107.2 0.4 copy.178
  107.7 1.3 fusion.6
  109.2 5.6 %fusion.38 = f32[512,4096]{1,0:T(8,128)} fusion(bf16[4096,512]{1,0:T(8,128)(2,1)S(1)} %copy-done.8, bf16[64,8,4,128]{3,2,1,0:T(4,128)(2,1)S(1)} %bitcast.165), kind=kOutput, calls=%fused_computation.81 | convolution fusion | flops 2147483648 | bytes 13107200 | tf_op jit(solution)/shard_map/dot_general | solution.py:121
  114.8 1.1 reduce_sum.51
  117.3 5.2 %fusion.39 = f32[512,4096]{1,0:T(8,128)S(1)} fusion(bf16[4096,512]{1,0:T(8,128)(2,1)} %param.13, bf16[64,8,4,128]{3,2,1,0:T(4,128)(2,1)S(1)} %bitcast.167), kind=kOutput, calls=%fused_computation.82 | convolution fusion | flops 2147483648 | bytes 13107200 | tf_op jit(solution)/shard_map/dot_general | solution.py:121
  122.5 8.1 %add_add_fusion = f32[512,4096]{1,0:T(8,128)} fusion(f32[512,4096]{1,0:T(8,128)S(1)} %bitcast.156, f32[512,4096]{1,0:T(8,128)S(1)} %fusion.39, bf16[4096,512]{1,0:T(8,128)(2,1)} %param.14, bf16[64,8,4,128]{3,2,1,0:T(4,128)(2,1)S(1)} %bitcast.161), kind=kOutput, calls=%fused_computation.3 | convolution fusion | flops 2151677952 | bytes 29884416 | tf_op jit(solution)/shard_map/dot_general | solution.py:121
  130.9 0.7 copy-done.1
  132.0 12.0 %fusion = bf16[4096,1536]{0,1:T(8,128)(2,1)} fusion(bf16[512,4096]{1,0:T(8,128)(2,1)} %param.11, bf16[512,512]{1,0:T(8,128)(2,1)S(1)} %get-tuple-element.69, bf16[512,512]{1,0:T(8,128)(2,1)S(1)} %get-tuple-element.70, bf16[512,512]{1,0:T(8,128)(2,1)S(1)} %bitcast.175), kind=kOutput, calls=%fused_computation.1 | convolution fusion | flops 6453460992 | bytes 18350080 | tf_op jit(solution)/shard_map/dot_general | solution.py:127
  144.0 4.7 %convolution_convert_fusion.1 = bf16[512,4096]{1,0:T(8,128)(2,1)S(1)} fusion(bf16[512,4096]{1,0:T(8,128)(2,1)} %all-gather.2.cloned.1.call-done, bf16[64,8,4,128]{3,2,1,0:T(4,128)(2,1)S(1)} %bitcast.164), kind=kOutput, calls=%fused_computation.4 | convolution fusion | flops 2149580800 | bytes 8912896 | tf_op jit(solution)/shard_map/dot_general | solution.py:223
  148.7 2.5 copy.262
  151.1 6.6 %all-to-all-start.1 = ((bf16[16,512,256]{2,1,0:T(8,128)(2,1)}), bf16[16,512,256]{2,1,0:T(8,128)(2,1)}, u32[]{:S(2)}, u32[]{:S(2)}) async-start(bf16[16,512,256]{2,1,0:T(8,128)(2,1)} %bitcast.159), calls=%async_computation.4 | async-start | bytes 8388608 | tf_op jit(solution)/shard_map/all_to_all | solution.py:36
  157.8 46.6 %all-to-all-done.1 = bf16[16,512,256]{2,1,0:T(8,128)(2,1)} async-done(((bf16[16,512,256]{2,1,0:T(8,128)(2,1)}), bf16[16,512,256]{2,1,0:T(8,128)(2,1)}, u32[]{:S(2)}, u32[]{:S(2)}) %all-to-all-start.1) | async-done | bytes 4194336 | tf_op jit(solution)/shard_map/all_to_all | solution.py:36
  204.4 3.6 %convert_reduce_fusion = f32[512,256]{1,0:T(8,128)} fusion(bf16[16,512,256]{2,1,0:T(8,128)(2,1)} %all-to-all-done.1), kind=kLoop, calls=%fused_computation.2 | loop fusion | flops 4063232 | bytes 4718592 | tf_op jit(solution)/shard_map/reduce_sum | solution.py:37
  208.0 2.3 add_convert_fusion.1
  210.3 2.2 add_convert_fusion
  212.5 85.3 %reduce-scatter.8.cloned.1.call-done = bf16[256,1536]{0,1:T(8,128)(2,1)} async-done(((bf16[4096,1536]{0,1:T(8,128)(2,1)}), bf16[256,1536]{0,1:T(8,128)(2,1)}) %reduce-scatter.8.cloned.1.call-update) | async-done | bytes 786448 | tf_op jit(solution)/shard_map/reduce_scatter | solution.py:217
  297.8 1.2 fusion.42
  299.0 1.0 copy.191
  300.0 1.0 copy.190
  301.0 1.0 copy.189
  (103 shorter events, 6.1 us)
Async XLA Ops:
  7.2 62.2 %all-gather.2.cloned.1.call-start = ((), (), s32[]{:S(2)}) async-start(), calls=%async_computation.6 | async-start | bytes 4718592 | tf_op jit(solution)/shard_map/all_gather | solution.py:178
  7.9 200.1 %reduce-scatter.4.cloned.1.call-start = ((), (), s32[]{:S(2)}) async-start(), calls=%async_computation.5 | async-start | bytes 9437184 | tf_op jit(solution)/shard_map/reduce_scatter | solution.py:174
  19.9 46.5 %copy-start.9 = (bf16[8,64,4,128]{3,2,1,0:T(4,128)(2,1)}, bf16[8,64,4,128]{3,2,1,0:T(4,128)(2,1)S(1)}, u32[]{:S(2)}) copy-start(bf16[8,64,4,128]{3,2,1,0:T(4,128)(2,1)S(1)} %reshape.208) | copy-start | bytes 1572868
  41.6 24.2 %copy-start.15 = (bf16[128,512]{0,1:T(8,128)(2,1)}, bf16[128,512]{0,1:T(8,128)(2,1)S(1)}, u32[]{:S(2)}) copy-start(bf16[128,512]{0,1:T(8,128)(2,1)S(1)} %copy.154) | copy-start | bytes 393220
  41.6 24.0 %copy-start.24 = (s32[128]{0:T(128)S(1)}, s32[128]{0:T(128)}, u32[]{:S(2)}) copy-start(s32[128]{0:T(128)} %param.16) | copy-start | bytes 1540
  47.7 20.4 %copy-start.11 = (bf16[8,64,4,128]{3,2,1,0:T(4,128)(2,1)}, bf16[8,64,4,128]{3,2,1,0:T(4,128)(2,1)S(1)}, u32[]{:S(2)}) copy-start(bf16[8,64,4,128]{3,2,1,0:T(4,128)(2,1)S(1)} %reshape.206) | copy-start | bytes 1572868
  65.6 9.8 %copy-start.17 = (bf16[128,512]{0,1:T(8,128)(2,1)}, bf16[128,512]{0,1:T(8,128)(2,1)S(1)}, u32[]{:S(2)}) copy-start(bf16[128,512]{0,1:T(8,128)(2,1)S(1)} %copy.162) | copy-start | bytes 393220
  67.1 8.2 %copy-start.19 = (f32[8,64,4]{1,0,2:T(8,128)}, f32[8,64,4]{1,0,2:T(8,128)S(1)}, u32[]{:S(2)}) copy-start(f32[8,64,4]{1,0,2:T(8,128)S(1)} %bitcast_maximum_fusion) | copy-start | bytes 24580
  67.8 7.6 %copy-start.21 = (f32[8,64,4]{1,0,2:T(8,128)}, f32[8,64,4]{1,0,2:T(8,128)S(1)}, u32[]{:S(2)}) copy-start(f32[8,64,4]{1,0,2:T(8,128)S(1)} %bitcast_add_fusion) | copy-start | bytes 24580
  75.3 3.5 %copy-start.7 = (bf16[512,4096]{1,0:T(8,128)(2,1)S(1)}, bf16[512,4096]{1,0:T(8,128)(2,1)}, u32[]{:S(2)}) copy-start(bf16[512,4096]{1,0:T(8,128)(2,1)} %param.15) | copy-start | bytes 12582916
  84.4 0.9 copy-start.20
  84.4 0.9 copy-start.22
  85.3 6.5 %copy-start.18 = (bf16[128,512]{0,1:T(8,128)(2,1)S(1)}, bf16[128,512]{0,1:T(8,128)(2,1)}, u32[]{:S(2)}) copy-start(bf16[128,512]{0,1:T(8,128)(2,1)} %copy-done.17) | copy-start | bytes 393220
  89.4 1.1 copy-start.4
  94.9 0.8 copy-start.12
  95.7 10.9 %copy-start.10 = (bf16[8,64,4,128]{3,2,1,0:T(4,128)(2,1)S(1)}, bf16[8,64,4,128]{3,2,1,0:T(4,128)(2,1)}, u32[]{:S(2)}) copy-start(bf16[8,64,4,128]{3,2,1,0:T(4,128)(2,1)} %copy-done.9) | copy-start | bytes 1572868
  95.7 11.3 %copy-start.16 = (bf16[128,512]{0,1:T(8,128)(2,1)S(1)}, bf16[128,512]{0,1:T(8,128)(2,1)}, u32[]{:S(2)}) copy-start(bf16[128,512]{0,1:T(8,128)(2,1)} %copy-done.15) | copy-start | bytes 393220
  96.7 10.2 %copy-start.13 = (bf16[8,64,4,128]{3,1,0,2:T(8,128)(2,1)S(1)}, bf16[8,64,4,128]{3,1,0,2:T(8,128)(2,1)}, u32[]{:S(2)}) copy-start(bf16[8,64,4,128]{3,1,0,2:T(8,128)(2,1)} %copy-done.12) | copy-start | bytes 1572868
  100.6 14.3 %all-to-all-start = ((f32[16,8,1024]{2,1,0:T(8,128)}), f32[16,8,1024]{2,1,0:T(8,128)}, u32[]{:S(2)}, u32[]{:S(2)}) async-start(f32[16,8,1024]{2,1,0:T(8,128)} %pad_maximum_fusion), calls=%async_computation.1 | async-start | bytes 1048576 | tf_op jit(solution)/shard_map/all_to_all | solution.py:23
  104.8 105.5 %reduce-scatter.6.cloned.1.call-start = ((), (), s32[]{:S(2)}) async-start(), calls=%async_computation.7 | async-start | bytes 9437184 | tf_op jit(solution)/shard_map/reduce_scatter | solution.py:214
  106.6 2.7 copy-start.8
  107.7 1.3 copy-start
  109.2 6.8 %copy-start.23 = (f32[8,4,128,1]{2,3,1,0:T(1,128)S(1)}, f32[8,4,128,1]{2,3,1,0:T(1,128)}, u32[]{:S(2)}) copy-start(f32[8,4,128,1]{2,3,1,0:T(1,128)} %slice.79) | copy-start | bytes 49156
  109.2 6.8 %copy-start.5 = (f32[8,4,128,64]{2,3,1,0:T(8,128)S(1)}, f32[8,4,128,64]{2,3,1,0:T(8,128)}, u32[]{:S(2)}) copy-start(f32[8,4,128,64]{2,3,1,0:T(8,128)} %copy-done.4) | copy-start | bytes 3145732
  109.2 7.4 %copy-start.6 = (f32[8,64,4,128]{3,1,2,0:T(8,128)S(1)}, f32[8,64,4,128]{3,1,2,0:T(8,128)}, u32[]{:S(2)}) copy-start(f32[8,64,4,128]{3,1,2,0:T(8,128)} %fusion.6) | copy-start | bytes 3145732
  116.8 5.7 %slice-start = ((s8[8388608]{0:T(1024)(128)(4,1)}), s8[4194304]{0:T(1024)(128)(4,1)S(1)}, s32[]{:S(2)}) async-start(s8[8388608]{0:T(1024)(128)(4,1)} %bitcast.155), calls=%async_computation.9 | async-start | bytes 8388608
  117.3 5.2 %copy-start.2 = (bf16[8,64,4,128]{3,2,1,0:T(4,128)(2,1)}, bf16[8,64,4,128]{3,2,1,0:T(4,128)(2,1)S(1)}, u32[]{:S(2)}) copy-start(bf16[8,64,4,128]{3,2,1,0:T(4,128)(2,1)S(1)} %copy.184) | copy-start | bytes 1572868
  117.3 5.2 %slice-start.1 = ((s8[8388608]{0:T(1024)(128)(4,1)}), s8[4194304]{0:T(1024)(128)(4,1)S(1)}, s32[]{:S(2)}) async-start(s8[8388608]{0:T(1024)(128)(4,1)} %bitcast.155), calls=%async_computation.10 | async-start | bytes 8388608
  130.6 1.1 copy-start.1
  130.6 1.2 copy-start.3
  130.6 167.2 %reduce-scatter.8.cloned.1.call-start = ((), (), s32[]{:S(2)}) async-start(), calls=%async_computation.8 | async-start | bytes 13369344 | tf_op jit(solution)/shard_map/reduce_scatter | solution.py:217
  151.1 53.2 %all-to-all-start.1 = ((bf16[16,512,256]{2,1,0:T(8,128)(2,1)}), bf16[16,512,256]{2,1,0:T(8,128)(2,1)}, u32[]{:S(2)}, u32[]{:S(2)}) async-start(bf16[16,512,256]{2,1,0:T(8,128)(2,1)} %bitcast.159), calls=%async_computation.4 | async-start | bytes 8388608 | tf_op jit(solution)/shard_map/all_to_all | solution.py:36
  157.7 52.5 %copy-start.14 = (bf16[512,512]{1,0:T(8,128)(2,1)S(1)}, bf16[512,512]{1,0:T(8,128)(2,1)}, u32[]{:S(2)}) copy-start(bf16[512,512]{1,0:T(8,128)(2,1)} %param.17) | copy-start | bytes 1572868
Sparse Core Ops, SparseCore 0:
  9.7 35.8 all-gather.1
  84.5 60.3 reduce-scatter.3
  147.4 52.1 reduce-scatter.5
  202.8 94.9 reduce-scatter.7
where the time goes:
time: 309 us
  waiting for transfers between devices  133 us (43%)
  matrix products  77.3 us (25%)
  blocking collectives  39.2 us (13%)
  local copies, waits for them, and re-layouts  18.9 us (6%)
  other arithmetic  14.5 us (5%)
  between operations  14.4 us (5%)
  starting transfers between devices  11.5 us (4%)
    reduce_scatter x1, waiting for transfers between devices, per_device(): lax.psum_scatter(term_maker(tokens, stacked).astype(jnp.bfloat16), 'ctx',...  85.3 us
    all_to_all x1, waiting for transfers between devices, sent_and_summed(): lax.all_to_all(cut_along(shard, dim, length), axis, 0, 0, tiled=True)  46.6 us
    dot_general x4, matrix products, back_project(): lax.dot_general(grad_rows, weight, (((1,), (1,)), ((), ())), preferred_el...  24.7 us
    all_gather x1, blocking collectives, per_device(): lax.all_gather(own_key, 'ctx', axis=0, tiled=True)  21.5 us
    all_gather x1, blocking collectives, per_device(): lax.all_gather(own_value, 'ctx', axis=0, tiled=True)  17.8 us
    dot_general x3, matrix products, project(): jnp.dot(tokens, weight, preferred_element_type=jnp.float32)  17.5 us
    dot_general x1, matrix products, term_maker(): lax.dot_general(tokens, grad_rows, (((0,), (0,)), ((), ())), preferred_el...  12 us
    dot_general x10, matrix products, elementwise_product(): jnp.einsum(pattern, left_side, right_side, preferred_element_type=jnp.flo...  11.3 us
  transfers between devices with their start and end apart: 6, of which 2 were waited for; matrix products, arithmetic and copies ran while one was open for 29% of the time, Pallas kernels for 0%

commit v1 on v0

--- a/solution.py
+++ b/solution.py
@@ -145,10 +145,9 @@
     value_row_matrix = project(w_value).reshape(block_shape)
     own_key = key_row_matrix[:, BLOCK - 1].reshape(blocks, col_count)
     own_value = value_row_matrix[:, BLOCK - 1].reshape(blocks, col_count)
-    summary_key, summary_value = (
-        lax.all_gather(own_key, "ctx", axis=0, tiled=True),
-        lax.all_gather(own_value, "ctx", axis=0, tiled=True),
-    )
+    own_both = jnp.concatenate([own_key, own_value], axis=1)
+    summary_both = lax.all_gather(own_both, "ctx", axis=0, tiled=True)
+    summary_key, summary_value = summary_both[:, :col_count], summary_both[:, col_count:]
     total_blocks = summary_key.shape[0]
     summary_key = summary_key.reshape(total_blocks, head_count, HDIM)
     summary_value = summary_value.reshape(total_blocks, head_count, HDIM)
@@ -171,7 +170,9 @@
     )
     attn = combined_output.reshape(tok_rows, col_count)
     partial_value = jnp.dot(attn, w_out, preferred_element_type=jnp.float32)
-    summed = lax.psum_scatter(partial_value, "tp", scatter_dimension=1, tiled=True)
+    summed = lax.psum_scatter(
+        partial_value.astype(jnp.bfloat16), "tp", scatter_dimension=1, tiled=True
+    ).astype(jnp.float32)
     shard_width = summed.shape[1]
     residual = lax.dynamic_slice_in_dim(tokens, lax.axis_index("tp") * shard_width, shard_width, 1)
     output = (residual.astype(jnp.float32) + summed).astype(jnp.bfloat16)
@@ -211,7 +212,9 @@
         + back_project(d_key, w_key)
         + back_project(d_value, w_value)
     )
-    d_summed = lax.psum_scatter(d_partial, "tp", scatter_dimension=1, tiled=True)
+    d_summed = lax.psum_scatter(
+        d_partial.astype(jnp.bfloat16), "tp", scatter_dimension=1, tiled=True
+    ).astype(jnp.float32)
     grad_tokens = (grad_out.astype(jnp.float32) + d_summed).astype(jnp.bfloat16)
     stacked = jnp.concatenate([query_gradient, d_key, d_value], axis=1)
     joined = lax.psum_scatter(

time: 309 us -> 289 us (0.935)
  blocking collectives: 39.2 us -> 21.6 us
  waiting for transfers between devices: 133 us -> 127 us
    all_gather x2 -> x1, blocking collectives: 39.2 us -> 21.6 us  [per_device(): summary_both = lax.all_gather(own_both, 'ctx', axis=0, tiled=True)]
    reduce_scatter x1, waiting for transfers between devices: 85.3 us -> 70.8 us  [per_device(): lax.psum_scatter(term_maker(tokens, stacked).astype(jnp.bfloat16), 'ctx',...]
    all_to_all x1, waiting for transfers between devices: 46.6 us -> 55.3 us  [sent_and_summed(): lax.all_to_all(cut_along(shard, dim, length), axis, 0, 0, tiled=True)]
    dot_general x4, matrix products: 24.7 us -> 29.5 us  [back_project(): lax.dot_general(grad_rows, weight, (((1,), (1,)), ((), ())), preferred_el...]
    unnamed x62 -> x46, local copies, waits for them, and re-layouts: 6.12 us -> 8.09 us
  transfers between devices with their start and end apart: 6 -> 6, of which waited for: 2 -> 2; matrix products, arithmetic and copies ran while one was open for 29% -> 31% of each run, Pallas kernels for 0% -> 0%
where the time goes in v1:
time: 289 us; the launch traced here: 288 us
  waiting for transfers between devices  127 us (44%)
  matrix products  79.7 us (28%)
  blocking collectives  21.6 us (7%)
  local copies, waits for them, and re-layouts  19.7 us (7%)
  between operations  14.3 us (5%)
  other arithmetic  13.2 us (5%)
  starting transfers between devices  12.4 us (4%)
    reduce_scatter x1, waiting for transfers between devices, per_device(): lax.psum_scatter(term_maker(tokens, stacked).astype(jnp.bfloat16), 'ctx',...  70.8 us
    all_to_all x1, waiting for transfers between devices, sent_and_summed(): lax.all_to_all(cut_along(shard, dim, length), axis, 0, 0, tiled=True)  55.3 us
    dot_general x4, matrix products, back_project(): lax.dot_general(grad_rows, weight, (((1,), (1,)), ((), ())), preferred_el...  29.5 us
    all_gather x1, blocking collectives, per_device(): summary_both = lax.all_gather(own_both, 'ctx', axis=0, tiled=True)  21.6 us
    dot_general x3, matrix products, project(): jnp.dot(tokens, weight, preferred_element_type=jnp.float32)  17.7 us
    dot_general x1, matrix products, term_maker(): lax.dot_general(tokens, grad_rows, (((0,), (0,)), ((), ())), preferred_el...  11.9 us
    dot_general x10, matrix products, elementwise_product(): jnp.einsum(pattern, left_side, right_side, preferred_element_type=jnp.flo...  9.62 us
    unnamed x46, local copies, waits for them, and re-layouts  8.09 us
  transfers between devices with their start and end apart: 6, of which 2 were waited for; matrix products, arithmetic and copies ran while one was open for 31% of the time, Pallas kernels for 0%

profile of v1, /device:TPU:1, one launch (start us, length us, event | category | flops | bytes accessed | tf_op | source)
XLA Modules:
  0.0 287.8 jit_solution(2680584412550340142)
XLA Ops:
  7.2 0.7 all-gather.2.cloned.1.call-update
  8.0 5.8 %convolution_convert_fusion.5 = bf16[512,512]{1,0:T(8,128)(2,1)S(1)} fusion(bf16[512,4096]{1,0:T(8,128)(2,1)} %param.11, bf16[4096,512]{1,0:T(8,128)(2,1)} %param.12), kind=kOutput, calls=%fused_computation.29 | convolution fusion | flops 2147745792 | bytes 8912896 | tf_op jit(solution)/shard_map/dot_general | solution.py:141
  14.0 5.8 %convolution_convert_fusion.4 = bf16[512,512]{1,0:T(8,128)(2,1)S(1)} fusion(bf16[512,4096]{1,0:T(8,128)(2,1)} %param.11, bf16[4096,512]{1,0:T(8,128)(2,1)} %param.13), kind=kOutput, calls=%fused_computation.28 | convolution fusion | flops 2147745792 | bytes 8912896 | tf_op jit(solution)/shard_map/dot_general | solution.py:141
  19.9 6.1 %convolution_convert_fusion.6 = bf16[512,512]{1,0:T(8,128)(2,1)S(1)} fusion(bf16[512,4096]{1,0:T(8,128)(2,1)} %param.11, bf16[4096,512]{1,0:T(8,128)(2,1)} %param.14), kind=kOutput, calls=%fused_computation.30 | convolution fusion | flops 2147745792 | bytes 8912896 | tf_op jit(solution)/shard_map/dot_general | solution.py:141
  26.3 21.6 %all_gather.6 = bf16[128,1024]{1,0:T(8,128)(2,1)S(1)} all-gather(bf16[8,1024]{1,0:T(8,128)(2,1)S(1)} %pad_maximum_fusion.1), channel_id=1, replica_groups=mesh['ctx'=16,'tp'=8] {'ctx'}, dimensions={0}, use_global_device_ids=true | all-gather | bytes 278528 | tf_op jit(solution)/shard_map/all_gather | solution.py:149
  49.0 0.4 fusion.44
  49.7 0.6 fusion.18
  50.6 1.3 convolution_bitcast_fusion.3
  51.9 6.6 %convolution_convert_fusion.3 = bf16[512,512]{1,0:T(8,128)(2,1)} fusion(bf16[512,4096]{1,0:T(8,128)(2,1)} %all-gather.2.cloned.1.call-done, bf16[512,4096]{1,0:T(8,128)(2,1)} %param.15), kind=kOutput, calls=%fused_computation.27 | convolution fusion | flops 2147745792 | bytes 8912896 | tf_op jit(solution)/shard_map/dot_general | solution.py:121
  58.6 1.2 reshape.212
  59.8 3.0 %multiply_reduce_fusion = (f32[8,64,4]{1,2,0:T(4,128)}, bf16[8,64,4,128]{3,1,2,0:T(8,128)(2,1)S(1)}) fusion(bf16[8,64,4,128]{3,2,1,0:T(4,128)(2,1)S(1)} %reshape.212, f32[8,64,4,128]{3,1,2,0:T(8,128)} %convolution_bitcast_fusion.3, bf16[128,4,128,1]{0,2,1,3:T(8,128)(2,1)S(1)} %bitcast.178, f32[8,64,4]{1,0,2:T(8,128)S(1)} %bitcast_add_fusion, ...), kind=kOutput, calls=%fused_computation.39 | convolution fusion | flops 69990400 | bytes 3302400 | tf_op jit(solution)/shard_map/gtuv,vuk->gtuk/dot_general | solution.py:41
  63.2 0.8 copy-done.7
  64.0 4.3 %convolution_convert_fusion.2 = bf16[512,4096]{1,0:T(8,128)(2,1)} fusion(bf16[512,4096]{1,0:T(8,128)(2,1)S(1)} %copy-done.15, bf16[64,8,4,128]{3,2,1,0:T(4,128)(2,1)S(1)} %bitcast.169), kind=kOutput, calls=%fused_computation.5 | convolution fusion | flops 2149580800 | bytes 8912896 | tf_op jit(solution)/shard_map/dot_general | solution.py:172
  68.3 0.9 copy.174
  69.2 1.8 convolution_bitcast_fusion.4
  71.1 1.1 copy.183
  72.2 0.8 concatenate.20
  73.3 1.1 copy-done
  74.3 0.6 slice.89
  75.0 0.7 copy.175
  75.7 1.3 fusion.46
  77.0 1.7 multiply_convert_fusion
  78.8 0.8 copy-done.4
  80.2 0.8 pad_maximum_fusion
  81.0 5.1 %all-to-all-start = ((f32[16,8,1024]{2,1,0:T(8,128)}), f32[16,8,1024]{2,1,0:T(8,128)}, u32[]{:S(2)}, u32[]{:S(2)}) async-start(f32[16,8,1024]{2,1,0:T(8,128)} %pad_maximum_fusion), calls=%async_computation.1 | async-start | bytes 1048576 | tf_op jit(solution)/shard_map/all_to_all | solution.py:23
  86.4 1.5 fusion.12
  88.6 0.4 copy.178
  89.3 0.9 copy-done.2
  90.2 5.6 %fusion.37 = f32[512,4096]{1,0:T(8,128)} fusion(bf16[4096,512]{1,0:T(8,128)(2,1)S(1)} %copy-done.2, bf16[64,8,4,128]{3,2,1,0:T(4,128)(2,1)S(1)} %bitcast.161), kind=kOutput, calls=%fused_computation.82 | convolution fusion | flops 2147483648 | bytes 13107200 | tf_op jit(solution)/shard_map/dot_general | solution.py:121
  95.8 1.1 reduce_sum.51
  97.1 0.4 copy.187
  97.8 0.4 copy.184
  98.2 8.2 %fusion.38 = f32[512,4096]{1,0:T(8,128)} fusion(bf16[4096,512]{1,0:T(8,128)(2,1)} %param.13, bf16[64,8,4,128]{3,2,1,0:T(4,128)(2,1)S(1)} %bitcast.165), kind=kOutput, calls=%fused_computation.83 | convolution fusion | flops 2147483648 | bytes 13107200 | tf_op jit(solution)/shard_map/dot_general | solution.py:121
  106.4 9.1 %add_convert_fusion = bf16[512,4096]{1,0:T(8,128)(2,1)} fusion(f32[512,4096]{1,0:T(8,128)S(1)} %bitcast.156, f32[512,4096]{1,0:T(8,128)} %fusion.38, bf16[4096,512]{1,0:T(8,128)(2,1)} %param.14, bf16[64,8,4,128]{3,2,1,0:T(4,128)(2,1)S(1)} %bitcast.163), kind=kOutput, calls=%fused_computation.3 | convolution fusion | flops 2153775104 | bytes 25690112 | tf_op jit(solution)/shard_map/dot_general | solution.py:121
  116.1 11.9 %fusion = bf16[4096,1536]{0,1:T(8,128)(2,1)} fusion(bf16[512,4096]{1,0:T(8,128)(2,1)} %param.11, bf16[512,512]{1,0:T(8,128)(2,1)S(1)} %bitcast.177, bf16[512,512]{1,0:T(8,128)(2,1)S(1)} %bitcast.176, bf16[512,512]{1,0:T(8,128)(2,1)S(1)} %bitcast.175), kind=kOutput, calls=%fused_computation.1 | convolution fusion | flops 6453460992 | bytes 18350080 | tf_op jit(solution)/shard_map/dot_general | solution.py:127
  128.1 1.0 copy-done.8
  129.1 4.9 %convolution_convert_fusion.1 = bf16[512,4096]{1,0:T(8,128)(2,1)S(1)} fusion(bf16[512,4096]{1,0:T(8,128)(2,1)} %all-gather.2.cloned.1.call-done, bf16[64,8,4,128]{3,2,1,0:T(4,128)(2,1)S(1)} %bitcast.170), kind=kOutput, calls=%fused_computation.4 | convolution fusion | flops 2149580800 | bytes 8912896 | tf_op jit(solution)/shard_map/dot_general | solution.py:226
  134.0 2.4 copy.264
  136.4 6.6 %all-to-all-start.1 = ((bf16[16,512,256]{2,1,0:T(8,128)(2,1)}), bf16[16,512,256]{2,1,0:T(8,128)(2,1)}, u32[]{:S(2)}, u32[]{:S(2)}) async-start(bf16[16,512,256]{2,1,0:T(8,128)(2,1)} %bitcast.159), calls=%async_computation.4 | async-start | bytes 8388608 | tf_op jit(solution)/shard_map/all_to_all | solution.py:36
  143.1 55.3 %all-to-all-done.1 = bf16[16,512,256]{2,1,0:T(8,128)(2,1)} async-done(((bf16[16,512,256]{2,1,0:T(8,128)(2,1)}), bf16[16,512,256]{2,1,0:T(8,128)(2,1)}, u32[]{:S(2)}, u32[]{:S(2)}) %all-to-all-start.1) | async-done | bytes 4194336 | tf_op jit(solution)/shard_map/all_to_all | solution.py:36
  198.3 3.7 %convert_reduce_fusion = f32[512,256]{1,0:T(8,128)} fusion(bf16[16,512,256]{2,1,0:T(8,128)(2,1)} %all-to-all-done.1), kind=kLoop, calls=%fused_computation.2 | loop fusion | flops 4063232 | bytes 4718592 | tf_op jit(solution)/shard_map/reduce_sum | solution.py:37
  202.0 2.1 add_convert_fusion.2
  204.1 2.0 add_convert_fusion.1
  206.1 70.8 %reduce-scatter.8.cloned.1.call-done = bf16[256,1536]{0,1:T(8,128)(2,1)} async-done(((bf16[4096,1536]{0,1:T(8,128)(2,1)}), bf16[256,1536]{0,1:T(8,128)(2,1)}) %reduce-scatter.8.cloned.1.call-update) | async-done | bytes 786448 | tf_op jit(solution)/shard_map/reduce_scatter | solution.py:220
  277.0 1.2 fusion.41
  278.2 1.0 copy.191
  279.2 1.0 copy.190
  280.2 1.0 copy.189
  (86 shorter events, 5.7 us)
Async XLA Ops:
  7.2 44.8 %all-gather.2.cloned.1.call-start = ((), (), s32[]{:S(2)}) async-start(), calls=%async_computation.6 | async-start | bytes 4718592 | tf_op jit(solution)/shard_map/all_gather | solution.py:179
  7.9 194.1 %reduce-scatter.4.cloned.1.call-start = ((), (), s32[]{:S(2)}) async-start(), calls=%async_computation.5 | async-start | bytes 4718592 | tf_op jit(solution)/shard_map/reduce_scatter | solution.py:173
  19.9 28.3 %copy-start.14 = (s32[128]{0:T(128)S(1)}, s32[128]{0:T(128)}, u32[]{:S(2)}) copy-start(s32[128]{0:T(128)} %param.16) | copy-start | bytes 1540
  26.2 24.4 %copy-start.3 = (bf16[8,64,4,128]{3,2,1,0:T(4,128)(2,1)}, bf16[8,64,4,128]{3,2,1,0:T(4,128)(2,1)S(1)}, u32[]{:S(2)}) copy-start(bf16[8,64,4,128]{3,2,1,0:T(4,128)(2,1)S(1)} %reshape.206) | copy-start | bytes 1572868
  48.1 11.7 %copy-start.10 = (bf16[128,512]{0,1:T(8,128)(2,1)}, bf16[128,512]{0,1:T(8,128)(2,1)S(1)}, u32[]{:S(2)}) copy-start(bf16[128,512]{0,1:T(8,128)(2,1)S(1)} %copy.204) | copy-start | bytes 393220
  48.4 20.8 %copy-start.13 = (pred[8,128]{1,0:T(8,128)(4,1)}, pred[8,128]{1,0:T(8,128)(4,1)S(1)}, u32[]{:S(2)}) copy-start(pred[8,128]{1,0:T(8,128)(4,1)S(1)} %fusion.35) | copy-start | bytes 3076
  50.4 18.9 %copy-start.11 = (f32[8,64,4]{1,0,2:T(8,128)}, f32[8,64,4]{1,0,2:T(8,128)S(1)}, u32[]{:S(2)}) copy-start(f32[8,64,4]{1,0,2:T(8,128)S(1)} %bitcast_add_fusion) | copy-start | bytes 24580
  59.7 4.2 %copy-start.15 = (bf16[512,4096]{1,0:T(8,128)(2,1)S(1)}, bf16[512,4096]{1,0:T(8,128)(2,1)}, u32[]{:S(2)}) copy-start(bf16[512,4096]{1,0:T(8,128)(2,1)} %param.15) | copy-start | bytes 12582916
  63.2 0.8 copy-start.7
  73.0 7.2 %copy-start.9 = (f32[16,8,512]{2,1,0:T(8,128)S(1)}, f32[16,8,512]{2,1,0:T(8,128)}, u32[]{:S(2)}) copy-start(f32[16,8,512]{2,1,0:T(8,128)} %concatenate.20) | copy-start | bytes 786436
  73.3 1.1 copy-start
  78.8 0.8 copy-start.4
  79.9 8.3 %copy-start.5 = (bf16[8,64,4,128]{3,1,0,2:T(8,128)(2,1)S(1)}, bf16[8,64,4,128]{3,1,0,2:T(8,128)(2,1)}, u32[]{:S(2)}) copy-start(bf16[8,64,4,128]{3,1,0,2:T(8,128)(2,1)} %copy-done.4) | copy-start | bytes 1572868
  81.0 14.7 %all-to-all-start = ((f32[16,8,1024]{2,1,0:T(8,128)}), f32[16,8,1024]{2,1,0:T(8,128)}, u32[]{:S(2)}, u32[]{:S(2)}) async-start(f32[16,8,1024]{2,1,0:T(8,128)} %pad_maximum_fusion), calls=%async_computation.1 | async-start | bytes 1048576 | tf_op jit(solution)/shard_map/all_to_all | solution.py:23
  86.1 118.0 %reduce-scatter.6.cloned.1.call-start = ((), (), s32[]{:S(2)}) async-start(), calls=%async_computation.7 | async-start | bytes 4718592 | tf_op jit(solution)/shard_map/reduce_scatter | solution.py:215
  87.9 2.3 copy-start.2
  90.2 6.7 %copy-start.12 = (f32[8,4,128,1]{2,3,1,0:T(1,128)S(1)}, f32[8,4,128,1]{2,3,1,0:T(1,128)}, u32[]{:S(2)}) copy-start(f32[8,4,128,1]{2,3,1,0:T(1,128)} %slice.89) | copy-start | bytes 49156
  90.2 6.8 %copy-start.1 = (f32[8,4,128,64]{2,3,1,0:T(8,128)S(1)}, f32[8,4,128,64]{2,3,1,0:T(8,128)}, u32[]{:S(2)}) copy-start(f32[8,4,128,64]{2,3,1,0:T(8,128)} %copy-done) | copy-start | bytes 3145732
  97.7 8.7 %slice-start = ((s8[8388608]{0:T(1024)(128)(4,1)}), s8[4194304]{0:T(1024)(128)(4,1)S(1)}, s32[]{:S(2)}) async-start(s8[8388608]{0:T(1024)(128)(4,1)} %bitcast.155), calls=%async_computation.9 | async-start | bytes 8388608
  98.2 8.2 %slice-start.1 = ((s8[8388608]{0:T(1024)(128)(4,1)}), s8[4194304]{0:T(1024)(128)(4,1)S(1)}, s32[]{:S(2)}) async-start(s8[8388608]{0:T(1024)(128)(4,1)} %bitcast.155), calls=%async_computation.10 | async-start | bytes 8388608
  115.5 161.5 %reduce-scatter.8.cloned.1.call-start = ((), (), s32[]{:S(2)}) async-start(), calls=%async_computation.8 | async-start | bytes 13369344 | tf_op jit(solution)/shard_map/reduce_scatter | solution.py:220
  128.0 1.0 copy-start.8
  136.4 61.9 %all-to-all-start.1 = ((bf16[16,512,256]{2,1,0:T(8,128)(2,1)}), bf16[16,512,256]{2,1,0:T(8,128)(2,1)}, u32[]{:S(2)}, u32[]{:S(2)}) async-start(bf16[16,512,256]{2,1,0:T(8,128)(2,1)} %bitcast.159), calls=%async_computation.4 | async-start | bytes 8388608 | tf_op jit(solution)/shard_map/all_to_all | solution.py:36
  143.1 61.1 %copy-start.6 = (bf16[512,512]{1,0:T(8,128)(2,1)S(1)}, bf16[512,512]{1,0:T(8,128)(2,1)}, u32[]{:S(2)}) copy-start(bf16[512,512]{1,0:T(8,128)(2,1)} %param.17) | copy-start | bytes 1572868
Sparse Core Ops, SparseCore 0:
  9.7 35.8 all-gather.1
  68.4 39.3 reduce-scatter.3
  115.7 40.8 reduce-scatter.5
  159.9 117.0 reduce-scatter.7

commit v2 on v0

v2 whole, which is shorter than its diff:
```python
import functools
import math

import jax
import jax.numpy as jnp
from jax import lax
from jax.experimental import pallas as pl
from jax.experimental.pallas import tpu as pltpu
from jax.sharding import PartitionSpec as P

HDIM = 128
BLOCK = 64
PAIR = 2 * BLOCK
MESH = pl.DeviceIdType.MESH
BF = jnp.bfloat16
F32 = jnp.float32
big_negative = -1e30


def dot_nn(a, b):
    return lax.dot_general(a, b, (((1,), (0,)), ((), ())), preferred_element_type=F32)


def dot_nt(a, b):
    return lax.dot_general(a, b, (((1,), (1,)), ((), ())), preferred_element_type=F32)


def dot_tn(a, b):
    return lax.dot_general(a, b, (((0,), (0,)), ((), ())), preferred_element_type=F32)


def iota(shape, dim):
    return lax.broadcasted_iota(jnp.int32, shape, dim)


def one_hot(hit):
    return jnp.where(hit, 1.0, 0.0).astype(BF)


def core_kernel(
    nctx,
    ntp,
    tok_h,
    wq_h,
    wk_h,
    wv_h,
    wo_h,
    doc_ref,
    go_h,
    attn_o,
    dq_o,
    dk_o,
    dv_o,
    gf_o,
    tok,
    w3,
    wo,
    qkv,
    gfull,
    land,
    lk,
    lv,
    pw,
    attn,
    da,
    dqv,
    dkv,
    dvv,
    dkf,
    dvf,
    dlk,
    dlv,
    dls,
    dlr,
    ld,
    st,
    g_s,
    g_r,
    f_s,
    l_s,
    l_r,
    d_s,
    d_r,
):
    ctx = lax.axis_index("ctx")
    tp = lax.axis_index("tp")
    nz = ntp // 2
    core = lax.rem(tp, 2)
    z = lax.div(tp, 2)
    partner = tp + 1 - 2 * core
    rows, width = tok.shape
    cols = qkv.shape[2]
    heads = cols // HDIM
    own_blocks = rows // BLOCK
    all_blocks = nctx * own_blocks
    per = 2 * own_blocks
    scale = 1.0 / math.sqrt(HDIM)

    def shard(t):
        return pl.ds(pl.multiple_of(t * cols, cols), cols)

    def mate(j, side):
        return lax.rem(z + j, nz) * 2 + side

    load_tok = pltpu.make_async_copy(tok_h, tok, ld.at[0])
    load_tok.start()
    for i, w_h in enumerate((wk_h, wv_h, wq_h)):
        pltpu.make_async_copy(w_h, w3.at[i], ld.at[1 + i]).start()
    load_wo = pltpu.make_async_copy(wo_h, wo, ld.at[4])
    load_wo.start()
    load_go = pltpu.make_async_copy(go_h, gfull.at[:, shard(tp)], ld.at[5])
    load_go.start()

    barrier = pltpu.get_barrier_semaphore()

    def greet(i, carry):
        pl.semaphore_signal(
            barrier, inc=1, device_id={"ctx": lax.rem(ctx + i, nctx)}, device_id_type=MESH
        )
        return carry

    lax.fori_loop(1, nctx, greet, 0)
    pl.semaphore_signal(barrier, inc=1, device_id={"tp": partner}, device_id_type=MESH)
    for j in range(1, nz):
        pl.semaphore_signal(barrier, inc=1, device_id={"tp": mate(j, core)}, device_id_type=MESH)
    pl.semaphore_wait(barrier, nctx - 1 + nz)

    def grad_copy(source, owner, send, target):
        return pltpu.make_async_remote_copy(
            src_ref=source,
            dst_ref=gfull.at[:, shard(owner)],
            send_sem=send,
            recv_sem=g_r.at[owner],
            device_id={"tp": target},
            device_id_type=MESH,
        )

    first_sends = [grad_copy(go_h, tp, g_s.at[j - 1], mate(j, core)) for j in range(1, nz)]
    first_sends.append(grad_copy(go_h, tp, g_s.at[nz - 1], partner))
    for send in first_sends:
        send.start()

    load_tok.wait()

    half = cols // 2

    def project(i, carry):
        pltpu.make_async_copy(wk_h, w3.at[i], ld.at[1 + i]).wait()

        def piece(n, inner):
            at = pl.ds(pl.multiple_of(n * half, half), half)
            qkv[i, :, at] = dot_nn(tok[...], w3[i, :, at]).astype(BF)
            return inner

        lax.fori_loop(0, 2, piece, 0)

        @pl.when(i == 1)
        def _():
            r = iota((per, rows), 0)
            c = iota((per, rows), 1)
            pick_k = one_hot(c == r * BLOCK + BLOCK - 1)
            pick_v = one_hot(c == (r - own_blocks) * BLOCK + BLOCK - 1)
            pick_k = jnp.where(r < own_blocks, pick_k, jnp.zeros_like(pick_k))
            pick_v = jnp.where(r >= own_blocks, pick_v, jnp.zeros_like(pick_v))
            land[ctx] = (dot_nn(pick_k, qkv[0]) + dot_nn(pick_v, qkv[1])).astype(BF)

            def spread(j, inner):
                pltpu.make_async_remote_copy(
                    src_ref=land.at[ctx],
                    dst_ref=land.at[ctx],
                    send_sem=l_s.at[j - 1],
                    recv_sem=l_r.at[ctx],
                    device_id={"ctx": lax.rem(ctx + j, nctx)},
                    device_id_type=MESH,
                ).start()
                return inner

            lax.fori_loop(1, nctx, spread, 0)

        return carry

    lax.fori_loop(0, 3, project, 0)

    def land_wait(j, carry):
        source = lax.rem(ctx + j, nctx)
        copy = pltpu.make_async_remote_copy(
            src_ref=land.at[ctx],
            dst_ref=land.at[source],
            send_sem=l_s.at[j - 1],
            recv_sem=l_r.at[source],
            device_id={"ctx": source},
            device_id_type=MESH,
        )
        copy.wait_send()
        copy.wait_recv()
        return carry

    lax.fori_loop(1, nctx, land_wait, 0)

    b = iota((all_blocks, nctx * per), 0)
    c = iota((all_blocks, nctx * per), 1)
    shift = b // own_blocks * own_blocks
    landed = land[...].reshape(nctx * per, cols)
    lk[...] = dot_nn(one_hot(c == b + shift), landed).astype(BF)
    lv[...] = dot_nn(one_hot(c == b + shift + own_blocks), landed).astype(BF)

    span = PAIR + all_blocks
    doc = doc_ref[...]
    doc_lane = iota(doc.shape, 1)
    doc_wide = jnp.concatenate([jnp.zeros((1, PAIR), jnp.int32), doc], axis=1)

    def forward(sb, carry):
        at = pl.ds(pl.multiple_of(sb * PAIR, PAIR), PAIR)
        row = iota((PAIR, span), 0)
        col = iota((PAIR, span), 1)
        upper = jnp.where(row >= BLOCK, 1, 0)
        col_upper = jnp.where(col >= BLOCK, 1, 0)
        first = ctx * own_blocks + sb * 2
        doc_a = jnp.sum(jnp.where(doc_lane == first, doc, 0), axis=1, keepdims=True)
        doc_b = jnp.sum(jnp.where(doc_lane == first + 1, doc, 0), axis=1, keepdims=True)
        own_doc = jnp.where(row >= BLOCK, doc_b, doc_a)
        near = (col < PAIR) & (upper == col_upper) & (col <= row)
        far = (col >= PAIR) & (col - PAIR < first + upper) & (doc_wide == own_doc)
        mask = near | far
        for h in range(heads):
            hs = pl.ds(h * HDIM, HDIM)
            keys = jnp.concatenate([qkv[0, at, hs], lk[:, hs]], axis=0)
            values = jnp.concatenate([qkv[1, at, hs], lv[:, hs]], axis=0)
            scores = dot_nt(qkv[2, at, hs], keys) * scale
            scores = jnp.where(mask, scores, big_negative)
            top = jnp.max(scores, axis=1, keepdims=True)
            e = jnp.exp(scores - top)
            weight = (e / jnp.sum(e, axis=1, keepdims=True)).astype(BF)
            pw[sb * heads + h] = weight
            attn[at, hs] = dot_nn(weight, values).astype(BF)
        return carry

    lax.fori_loop(0, rows // PAIR, forward, 0)
    out_attn = pltpu.make_async_copy(attn, attn_o, st.at[0])
    out_attn.start()

    forwards = []
    for j in range(1, nz):
        owner = mate(j, core)
        grad_copy(gfull.at[:, shard(owner)], owner, f_s.at[j - 1], partner).wait_recv()
        onward = grad_copy(gfull.at[:, shard(owner)], owner, f_s.at[j - 1], partner)
        onward.start()
        forwards.append(onward)
    grad_copy(go_h, partner, g_s.at[nz - 1], partner).wait_recv()
    for j in range(1, nz):
        owner = mate(j, 1 - core)
        grad_copy(gfull.at[:, shard(owner)], owner, f_s.at[j - 1], partner).wait_recv()
    load_go.wait()
    load_wo.wait()
    out_gf = pltpu.make_async_copy(gfull, gf_o, st.at[4])
    out_gf.start()

    def d_piece(n, carry):
        at = pl.ds(pl.multiple_of(n * half, half), half)
        da[:, at] = dot_nt(gfull[...], wo[at, :]).astype(BF)
        return carry

    lax.fori_loop(0, 2, d_piece, 0)

    dlk[...] = jnp.zeros_like(dlk)
    dlv[...] = jnp.zeros_like(dlv)

    def backward(sb, carry):
        at = pl.ds(pl.multiple_of(sb * PAIR, PAIR), PAIR)
        for h in range(heads):
            hs = pl.ds(h * HDIM, HDIM)
            keys = jnp.concatenate([qkv[0, at, hs], lk[:, hs]], axis=0)
            values = jnp.concatenate([qkv[1, at, hs], lv[:, hs]], axis=0)
            weight = pw[sb * heads + h]
            d_out = da[at, hs]
            delta = jnp.sum(
                attn[at, hs].astype(F32) * d_out.astype(F32), axis=1, keepdims=True
            )
            d_weight = dot_nt(d_out, values)
            ds = (weight.astype(F32) * (d_weight - delta)).astype(BF)
            dqv[at, hs] = (dot_nn(ds, keys) * scale).astype(BF)
            d_keys = dot_tn(ds, qkv[2, at, hs]) * scale
            d_values = dot_tn(weight, d_out)
            dkf[at, hs] = d_keys[:PAIR]
            dvf[at, hs] = d_values[:PAIR]
            dlk[:, hs] += d_keys[PAIR:]
            dlv[:, hs] += d_values[PAIR:]
        return carry

    lax.fori_loop(0, rows // PAIR, backward, 0)
    out_dq = pltpu.make_async_copy(dqv, dq_o, st.at[1])
    out_dq.start()

    r = iota((nctx * per, all_blocks), 0)
    b = iota((nctx * per, all_blocks), 1)
    shift = b // own_blocks * own_blocks
    packed = dot_nn(one_hot(r == b + shift), dlk[...].astype(BF)) + dot_nn(
        one_hot(r == b + shift + own_blocks), dlv[...].astype(BF)
    )
    dls[...] = packed.astype(BF).reshape(nctx, per, cols)

    def give(j, carry):
        target = lax.rem(ctx + j, nctx)
        pltpu.make_async_remote_copy(
            src_ref=dls.at[target],
            dst_ref=dlr.at[ctx],
            send_sem=d_s.at[j - 1],
            recv_sem=d_r.at[ctx],
            device_id={"ctx": target},
            device_id_type=MESH,
        ).start()
        return carry

    lax.fori_loop(1, nctx, give, 0)
    dlr[ctx] = dls[ctx]

    def take(j, carry):
        source = lax.rem(ctx + j, nctx)
        copy = pltpu.make_async_remote_copy(
            src_ref=dls.at[source],
            dst_ref=dlr.at[source],
            send_sem=d_s.at[j - 1],
            recv_sem=d_r.at[source],
            device_id={"ctx": source},
            device_id_type=MESH,
        )
        copy.wait_send()
        copy.wait_recv()
        return carry

    lax.fori_loop(1, nctx, take, 0)
    total = jnp.zeros((per, cols), F32)
    for i in range(nctx):
        total = total + dlr[i].astype(F32)
    for i in range(own_blocks):
        last = pl.ds(i * BLOCK + BLOCK - 1, 1)
        dkf[last, :] += total[i : i + 1]
        dvf[last, :] += total[own_blocks + i : own_blocks + i + 1]
    dkv[...] = dkf[...].astype(BF)
    dvv[...] = dvf[...].astype(BF)
    out_dk = pltpu.make_async_copy(dkv, dk_o, st.at[2])
    out_dk.start()
    out_dv = pltpu.make_async_copy(dvv, dv_o, st.at[3])
    out_dv.start()
    for send in first_sends + forwards:
        send.wait_send()
    for copy in (out_attn, out_dq, out_dk, out_dv, out_gf):
        copy.wait()


def attention_core(nctx, ntp, tokens, w_query, w_key, w_value, w_out, block_doc, grad_out):
    rows, width = tokens.shape
    cols = w_query.shape[1]
    heads = cols // HDIM
    own_blocks = rows // BLOCK
    all_blocks = nctx * own_blocks
    per = 2 * own_blocks
    units = rows // PAIR * heads
    small = jax.ShapeDtypeStruct((rows, cols), BF)
    hbm = pl.BlockSpec(memory_space=pl.ANY)
    dma = pltpu.SemaphoreType.DMA
    return pl.pallas_call(
        functools.partial(core_kernel, nctx, ntp),
        out_shape=(small, small, small, small, jax.ShapeDtypeStruct((rows, width), BF)),
        in_specs=[hbm] * 5 + [pl.BlockSpec(memory_space=pltpu.VMEM), hbm],
        out_specs=(hbm,) * 5,
        scratch_shapes=[
            pltpu.VMEM((rows, width), BF),
            pltpu.VMEM((3, width, cols), BF),
            pltpu.VMEM((cols, width), BF),
            pltpu.VMEM((3, rows, cols), BF),
            pltpu.VMEM((rows, width), BF),
            pltpu.VMEM((nctx, per, cols), BF),
            pltpu.VMEM((all_blocks, cols), BF),
            pltpu.VMEM((all_blocks, cols), BF),
            pltpu.VMEM((units, PAIR, PAIR + all_blocks), BF),
            pltpu.VMEM((rows, cols), BF),
            pltpu.VMEM((rows, cols), BF),
            pltpu.VMEM((rows, cols), BF),
            pltpu.VMEM((rows, cols), BF),
            pltpu.VMEM((rows, cols), BF),
            pltpu.VMEM((rows, cols), F32),
            pltpu.VMEM((rows, cols), F32),
            pltpu.VMEM((all_blocks, cols), F32),
            pltpu.VMEM((all_blocks, cols), F32),
            pltpu.VMEM((nctx, per, cols), BF),
            pltpu.VMEM((nctx, per, cols), BF),
            dma((6,)),
            dma((5,)),
            dma((ntp // 2,)),
            dma((ntp,)),
            dma((ntp // 2,)),
            dma((nctx - 1,)),
            dma((nctx,)),
            dma((nctx - 1,)),
            dma((nctx,)),
        ],
        compiler_params=pltpu.CompilerParams(
            collective_id=1, has_side_effects=True, vmem_limit_bytes=64 * 1024 * 1024 - 65536
        ),
        name="attention_core",
    )(tokens, w_query, w_key, w_value, w_out, block_doc.reshape(1, -1), grad_out)


def cut_along(shard, dim, length):
    dims = shard.shape
    blocks = shard.reshape(*dims[:dim], length, dims[dim] // length, *dims[dim + 1 :])
    return jnp.moveaxis(blocks, dim, 0)


def sent_and_summed(shard, axis, dim):
    length = lax.axis_size(axis)
    blocks = lax.all_to_all(cut_along(shard, dim, length), axis, 0, 0, tiled=True)
    return jnp.sum(blocks.astype(jnp.float32), axis=0)


def per_device(nctx, ntp, tokens, w_query, w_key, w_value, w_out, block_doc, grad_out):
    col_count = w_query.shape[1]
    attn, d_query, d_key, d_value, upstream = attention_core(
        nctx, ntp, tokens, w_query, w_key, w_value, w_out, block_doc, grad_out
    )
    stacked = jnp.concatenate([d_query, d_key, d_value], axis=1)
    joined = lax.psum_scatter(
        dot_tn(tokens, stacked).astype(BF), "ctx", scatter_dimension=0, tiled=True
    ).astype(F32)
    grad_query_weight = joined[:, :col_count]
    grad_key_weight = joined[:, col_count : 2 * col_count]
    grad_value_weight = joined[:, 2 * col_count :]
    summed = lax.psum_scatter(
        dot_nn(attn, w_out).astype(BF), "tp", scatter_dimension=1, tiled=True
    ).astype(F32)
    shard_width = summed.shape[1]
    residual = lax.dynamic_slice_in_dim(tokens, lax.axis_index("tp") * shard_width, shard_width, 1)
    output = (residual.astype(F32) + summed).astype(BF)
    d_partial = dot_nt(d_query, w_query) + dot_nt(d_key, w_key) + dot_nt(d_value, w_value)
    d_summed = lax.psum_scatter(
        d_partial.astype(BF), "tp", scatter_dimension=1, tiled=True
    ).astype(F32)
    grad_tokens = (grad_out.astype(F32) + d_summed).astype(BF)
    grad_out_weight = sent_and_summed(dot_tn(attn, upstream).astype(BF), "ctx", 1)
    return (
        output,
        grad_tokens,
        grad_query_weight,
        grad_key_weight,
        grad_value_weight,
        grad_out_weight,
    )


def solution(mesh):
    in_specs = (
        P("ctx", None),
        P(None, "tp"),
        P(None, "tp"),
        P(None, "tp"),
        P("tp", None),
        P(),
        P("ctx", "tp"),
    )
    out_specs = (
        P("ctx", "tp"),
        P("ctx", "tp"),
        P("ctx", "tp"),
        P("ctx", "tp"),
        P("ctx", "tp"),
        P("tp", "ctx"),
    )
    return jax.shard_map(
        functools.partial(per_device, mesh.shape["ctx"], mesh.shape["tp"]),
        mesh=mesh,
        in_specs=in_specs,
        out_specs=out_specs,
        check_vma=False,
    )
```

time: 309 us -> 262 us (0.85)
  Pallas kernels: 0 us -> 50.2 us
  blocking collectives: 39.2 us -> 0 us
  matrix products: 77.3 us -> 41.6 us
  local copies, waits for them, and re-layouts: 18.9 us -> 8.62 us
  other arithmetic: 14.5 us -> 7.77 us
  starting transfers between devices: 11.5 us -> 5.76 us
    pallas_call x0 -> x1, Pallas kernels: none -> 50.2 us  [attention_core(): pl.pallas_call(functools.partial(core_kernel, nctx, ntp), out_shape=(smal...]
    all_gather x2 -> x0, blocking collectives: 39.2 us -> none  [the longest x1 21.5 us: per_device(): lax.all_gather(own_key, 'ctx', axis=0, tiled=True)]
    dot_general x20 -> x6, matrix products: 75.7 us -> 41.6 us  [the longest x3 18.3 us: dot_nt(): lax.dot_general(a, b, (((1,), (1,)), ((), ())), preferred_element_type=F32)]
    all_to_all x1, waiting for transfers between devices: 46.6 us -> 74.3 us  [sent_and_summed(): lax.all_to_all(cut_along(shard, dim, length), axis, 0, 0, tiled=True)]
    reduce_scatter x3, waiting for transfers between devices: 85.3 us -> 59.6 us  [the longest x1 59.6 us: per_device(): lax.psum_scatter(dot_tn(tokens, stacked).astype(BF), 'ctx', scatter_dimen...]
    all_to_all x1 -> x0, starting transfers between devices: 4.26 us -> none  [summed_on_arrival(): lax.all_to_all(cut_along(shard, dim, length), axis, 0, 0, tiled=True)]
    convert_element_type x6 -> x2, other arithmetic: 6.59 us -> 4.11 us  [the longest x1 2.13 us: per_device(): output = (residual.astype(F32) + summed).astype(BF)]
  transfers between devices with their start and end apart: 6 -> 4, of which waited for: 2 -> 2; matrix products, arithmetic and copies ran while one was open for 29% -> 17% of each run, Pallas kernels for 0% -> 0%
where the time goes in v2:
time: 262 us
  waiting for transfers between devices  134 us (51%)
  Pallas kernels  50.2 us (19%)
  matrix products  41.6 us (16%)
  between operations  13.8 us (5%)
  local copies, waits for them, and re-layouts  8.62 us (3%)
  other arithmetic  7.77 us (3%)
  starting transfers between devices  5.76 us (2%)
    all_to_all x1, waiting for transfers between devices, sent_and_summed(): lax.all_to_all(cut_along(shard, dim, length), axis, 0, 0, tiled=True)  74.3 us
    reduce_scatter x1, waiting for transfers between devices, per_device(): lax.psum_scatter(dot_tn(tokens, stacked).astype(BF), 'ctx', scatter_dimen...  59.6 us
    pallas_call x1, Pallas kernels, attention_core(): pl.pallas_call(functools.partial(core_kernel, nctx, ntp), out_shape=(smal...  50.2 us
    dot_general x3, matrix products, dot_nt(): lax.dot_general(a, b, (((1,), (1,)), ((), ())), preferred_element_type=F32)  18.3 us
    dot_general x2, matrix products, dot_tn(): lax.dot_general(a, b, (((0,), (0,)), ((), ())), preferred_element_type=F32)  16.7 us
    dot_general x1, matrix products, dot_nn(): lax.dot_general(a, b, (((1,), (0,)), ((), ())), preferred_element_type=F32)  6.64 us
    all_to_all x1, starting transfers between devices, sent_and_summed(): lax.all_to_all(cut_along(shard, dim, length), axis, 0, 0, tiled=True)  5.46 us
  transfers between devices with their start and end apart: 4, of which 2 were waited for; matrix products, arithmetic and copies ran while one was open for 17% of the time, Pallas kernels for 0%

profile of v2, /device:TPU:1, one launch (start us, length us, event | category | flops | bytes accessed | tf_op | source)
XLA Modules:
  0.0 261.7 jit_solution(14468697472456457389)
XLA Ops:
  7.2 0.0 reduce-scatter.4.cloned.1.call-start
  7.2 50.2 %attention_core.1 = (bf16[512,512]{1,0:T(8,128)(2,1)}, bf16[512,512]{1,0:T(8,128)(2,1)}, bf16[512,512]{1,0:T(8,128)(2,1)}, bf16[512,512]{1,0:T(8,128)(2,1)}, bf16[512,4096]{1,0:T(8,128)(2,1)}) custom-call(bf16[512,4096]{1,0:T(8,128)(2,1)} %tok_h.1, bf16[4096,512]{1,0:T(8,128)(2,1)} %wq_h.1, bf16[4096,512]{1,0:T(8,128)(2,1)} %wk_h.1, bf16[4096,512]{1,0:T(8,128)(2,1)} %wv_h.1, ...), custom_call_target="tpu_custom_call" | custom-call | tf_op jit(solution)/shard_map/attention_core/pallas_call | solution.py:362
  57.4 6.6 %convolution_convert_fusion.2 = bf16[512,4096]{1,0:T(8,128)(2,1)} fusion(bf16[512,512]{1,0:T(8,128)(2,1)} %get-tuple-element.11, bf16[512,4096]{1,0:T(8,128)(2,1)} %wo_h.1), kind=kOutput, calls=%fused_computation.5 | convolution fusion | flops 2149580800 | bytes 8912896 | tf_op jit(solution)/shard_map/dot_general | solution.py:21
  64.0 0.0 copy-start.4
  64.0 0.0 reduce-scatter.4.cloned.1.call-update
  64.1 0.0 reduce-scatter.6.cloned.1.call-start
  64.1 1.0 copy-done.4
  65.1 0.0 copy-start
  65.1 0.0 copy-start.5
  65.1 4.7 %fusion.8 = f32[512,4096]{1,0:T(8,128)S(1)} fusion(bf16[512,512]{1,0:T(8,128)(2,1)S(1)} %copy-done.4, bf16[4096,512]{1,0:T(8,128)(2,1)} %wq_h.1), kind=kOutput, calls=%fused_computation.16 | convolution fusion | flops 2147483648 | bytes 13107200 | tf_op jit(solution)/shard_map/dot_general | solution.py:25
  69.8 0.0 copy-done
  69.8 0.0 copy-done.5
  69.8 0.0 copy-start.1
  69.8 0.0 copy-start.6
  69.8 5.7 %fusion.9 = f32[512,4096]{1,0:T(8,128)} fusion(bf16[512,512]{1,0:T(8,128)(2,1)S(1)} %copy-done.5, bf16[4096,512]{1,0:T(8,128)(2,1)S(1)} %copy-done), kind=kOutput, calls=%fused_computation.17 | convolution fusion | flops 2147483648 | bytes 13107200 | tf_op jit(solution)/shard_map/dot_general | solution.py:25
  75.5 0.0 copy-done.1
  75.5 0.0 copy-done.6
  75.5 7.9 %add_convert_fusion = bf16[512,4096]{1,0:T(8,128)(2,1)} fusion(f32[512,4096]{1,0:T(8,128)S(1)} %fusion.8, f32[512,4096]{1,0:T(8,128)} %fusion.9, bf16[512,512]{1,0:T(8,128)(2,1)S(1)} %copy-done.6, bf16[4096,512]{1,0:T(8,128)(2,1)S(1)} %copy-done.1), kind=kOutput, calls=%fused_computation.3 | convolution fusion | flops 2153775104 | bytes 25690112 | tf_op jit(solution)/shard_map/dot_general | solution.py:25
  83.4 0.0 reduce-scatter.6.cloned.1.call-update
  83.4 0.2 reduce-scatter.8.cloned.1.call-start
  83.7 12.0 %fusion = bf16[4096,1536]{0,1:T(8,128)(2,1)} fusion(bf16[512,4096]{1,0:T(8,128)(2,1)} %tok_h.1, bf16[512,512]{1,0:T(8,128)(2,1)S(1)} %copy-done.6, bf16[512,512]{1,0:T(8,128)(2,1)S(1)} %copy-done.5, bf16[512,512]{1,0:T(8,128)(2,1)S(1)} %copy-done.4), kind=kOutput, calls=%fused_computation.1 | convolution fusion | flops 6453460992 | bytes 18350080 | tf_op jit(solution)/shard_map/dot_general | solution.py:29
  95.7 0.0 copy-start.3
  95.7 0.0 reduce-scatter.8.cloned.1.call-update
  95.7 1.0 copy-done.3
  96.7 4.6 %convolution_convert_fusion.1 = bf16[512,4096]{1,0:T(8,128)(2,1)S(1)} fusion(bf16[512,512]{1,0:T(8,128)(2,1)S(1)} %copy-done.3, bf16[512,4096]{1,0:T(8,128)(2,1)} %get-tuple-element.15), kind=kOutput, calls=%fused_computation.4 | convolution fusion | flops 2149580800 | bytes 8912896 | tf_op jit(solution)/shard_map/dot_general | solution.py:29
  101.4 2.4 copy.22
  103.8 5.5 %all-to-all-start = ((bf16[16,512,256]{2,1,0:T(8,128)(2,1)}), bf16[16,512,256]{2,1,0:T(8,128)(2,1)}, u32[]{:S(2)}, u32[]{:S(2)}) async-start(bf16[16,512,256]{2,1,0:T(8,128)(2,1)} %bitcast.21), calls=%async_computation.3 | async-start | bytes 8388608 | tf_op jit(solution)/shard_map/all_to_all | solution.py:413
  109.2 0.0 copy-start.2
  109.3 74.3 %all-to-all-done = bf16[16,512,256]{2,1,0:T(8,128)(2,1)} async-done(((bf16[16,512,256]{2,1,0:T(8,128)(2,1)}), bf16[16,512,256]{2,1,0:T(8,128)(2,1)}, u32[]{:S(2)}, u32[]{:S(2)}) %all-to-all-start) | async-done | bytes 4194336 | tf_op jit(solution)/shard_map/all_to_all | solution.py:413
  183.6 3.7 %convert_reduce_fusion = f32[512,256]{1,0:T(8,128)} fusion(bf16[16,512,256]{2,1,0:T(8,128)(2,1)} %all-to-all-done), kind=kLoop, calls=%fused_computation.2 | loop fusion | flops 4063232 | bytes 4718592 | tf_op jit(solution)/shard_map/reduce_sum | solution.py:414
  187.3 0.0 reduce-scatter.4.cloned.1.call-done
  187.3 2.1 add_convert_fusion.2
  189.4 0.0 reduce-scatter.6.cloned.1.call-done
  189.4 0.0 copy-done.2
  189.4 2.0 add_convert_fusion.1
  191.4 59.6 %reduce-scatter.8.cloned.1.call-done = bf16[256,1536]{0,1:T(8,128)(2,1)} async-done(((bf16[4096,1536]{0,1:T(8,128)(2,1)}), bf16[256,1536]{0,1:T(8,128)(2,1)}) %reduce-scatter.8.cloned.1.call-update) | async-done | bytes 786448 | tf_op jit(solution)/shard_map/reduce_scatter | solution.py:423
  251.0 1.2 fusion.7
  252.2 1.0 copy.19
  253.2 1.0 copy.18
  254.2 1.0 copy.17
Async XLA Ops:
  7.2 180.1 %reduce-scatter.4.cloned.1.call-start = ((), (), s32[]{:S(2)}) async-start(), calls=%async_computation.4 | async-start | bytes 4718592 | tf_op jit(solution)/shard_map/reduce_scatter | solution.py:429
  64.0 1.0 copy-start.4
  64.1 125.3 %reduce-scatter.6.cloned.1.call-start = ((), (), s32[]{:S(2)}) async-start(), calls=%async_computation.5 | async-start | bytes 4718592 | tf_op jit(solution)/shard_map/reduce_scatter | solution.py:436
  65.1 4.7 %copy-start = (bf16[4096,512]{1,0:T(8,128)(2,1)S(1)}, bf16[4096,512]{1,0:T(8,128)(2,1)}, u32[]{:S(2)}) copy-start(bf16[4096,512]{1,0:T(8,128)(2,1)} %wk_h.1) | copy-start | bytes 12582916
  65.1 4.7 %copy-start.5 = (bf16[512,512]{1,0:T(8,128)(2,1)S(1)}, bf16[512,512]{1,0:T(8,128)(2,1)}, u32[]{:S(2)}) copy-start(bf16[512,512]{1,0:T(8,128)(2,1)} %get-tuple-element.13) | copy-start | bytes 1572868
  69.8 5.7 %copy-start.1 = (bf16[4096,512]{1,0:T(8,128)(2,1)S(1)}, bf16[4096,512]{1,0:T(8,128)(2,1)}, u32[]{:S(2)}) copy-start(bf16[4096,512]{1,0:T(8,128)(2,1)} %wv_h.1) | copy-start | bytes 12582916
  69.8 5.7 %copy-start.6 = (bf16[512,512]{1,0:T(8,128)(2,1)S(1)}, bf16[512,512]{1,0:T(8,128)(2,1)}, u32[]{:S(2)}) copy-start(bf16[512,512]{1,0:T(8,128)(2,1)} %get-tuple-element.14) | copy-start | bytes 1572868
  83.4 167.5 %reduce-scatter.8.cloned.1.call-start = ((), (), s32[]{:S(2)}) async-start(), calls=%async_computation.6 | async-start | bytes 13369344 | tf_op jit(solution)/shard_map/reduce_scatter | solution.py:423
  95.7 1.1 copy-start.3
  103.8 79.8 %all-to-all-start = ((bf16[16,512,256]{2,1,0:T(8,128)(2,1)}), bf16[16,512,256]{2,1,0:T(8,128)(2,1)}, u32[]{:S(2)}, u32[]{:S(2)}) async-start(bf16[16,512,256]{2,1,0:T(8,128)(2,1)} %bitcast.21), calls=%async_computation.3 | async-start | bytes 8388608 | tf_op jit(solution)/shard_map/all_to_all | solution.py:413
  109.2 80.2 %copy-start.2 = (bf16[512,512]{1,0:T(8,128)(2,1)S(1)}, bf16[512,512]{1,0:T(8,128)(2,1)}, u32[]{:S(2)}) copy-start(bf16[512,512]{1,0:T(8,128)(2,1)} %go_h.1) | copy-start | bytes 1572868
Sparse Core Ops, SparseCore 0:
  64.2 34.2 reduce-scatter.3
  100.9 37.4 reduce-scatter.5
  141.9 109.0 reduce-scatter.7

commit v3 on v2

--- a/solution.py
+++ b/solution.py
@@ -40,6 +40,7 @@
 def core_kernel(
     nctx,
     ntp,
+    nx,
     tok_h,
     wq_h,
     wk_h,
@@ -51,7 +52,9 @@
     dq_o,
     dk_o,
     dv_o,
-    gf_o,
+    wos_o,
+    tx_o,
+    ty_o,
     tok,
     w3,
     wo,
@@ -72,6 +75,7 @@
     dlv,
     dls,
     dlr,
+    wos,
     ld,
     st,
     g_s,
@@ -81,8 +85,20 @@
     l_r,
     d_s,
     d_r,
+    tx_s,
+    tx_r,
+    ty_s,
+    ty_r,
+    t_l,
+    fx_s,
+    fx_r,
+    fy_s,
+    fy_r,
 ):
     ctx = lax.axis_index("ctx")
+    ny = nctx // nx
+    y = lax.div(ctx, nx)
+    x = lax.rem(ctx, nx)
     tp = lax.axis_index("tp")
     nz = ntp // 2
     core = lax.rem(tp, 2)
@@ -196,6 +212,63 @@
         return carry
 
     lax.fori_loop(1, nctx, land_wait, 0)
+
+    strip = width // nctx
+    own_half = pl.ds(pl.multiple_of(core * (rows // 2), rows // 2), rows // 2)
+
+    def strip_at(i):
+        return pl.ds(pl.multiple_of(i * strip, strip), strip)
+
+    def x_copy(j, i, owner):
+        return pltpu.make_async_remote_copy(
+            src_ref=tok.at[own_half, strip_at(i * nx + lax.rem(x + j, nx))],
+            dst_ref=tx_o.at[owner, own_half, strip_at(i)],
+            send_sem=tx_s.at[j - 1, i],
+            recv_sem=tx_r.at[owner, i],
+            device_id={"ctx": y * nx + lax.rem(x + j, nx)},
+            device_id_type=MESH,
+        )
+
+    def y_copy(j, owner):
+        there = lax.rem(y + j, ny)
+        return pltpu.make_async_remote_copy(
+            src_ref=tok.at[own_half, pl.ds(pl.multiple_of(there * nx * strip, strip), nx * strip)],
+            dst_ref=ty_o.at[owner, own_half],
+            send_sem=ty_s.at[j - 1],
+            recv_sem=ty_r.at[owner],
+            device_id={"ctx": there * nx + x},
+            device_id_type=MESH,
+        )
+
+    def pass_on(ref, owner, send, recv):
+        return pltpu.make_async_remote_copy(
+            src_ref=ref.at[owner, own_half],
+            dst_ref=ref.at[owner, own_half],
+            send_sem=send,
+            recv_sem=recv,
+            device_id={"tp": partner},
+            device_id_type=MESH,
+        )
+
+    for j in (1, 3, 2):
+        for i in range(ny):
+            x_copy(j, i, x).start()
+        y_copy(j, y).start()
+    own_strips = [
+        pltpu.make_async_copy(
+            tok.at[:, strip_at(i * nx + x)], tx_o.at[x, :, strip_at(i)], t_l.at[i]
+        )
+        for i in range(ny)
+    ]
+    own_strips.append(
+        pltpu.make_async_copy(
+            tok.at[:, pl.ds(pl.multiple_of(y * nx * strip, strip), nx * strip)],
+            ty_o.at[y],
+            t_l.at[ny],
+        )
+    )
+    for copy in own_strips:
+        copy.start()
 
     b = iota((all_blocks, nctx * per), 0)
     c = iota((all_blocks, nctx * per), 1)
@@ -252,8 +325,6 @@
         grad_copy(gfull.at[:, shard(owner)], owner, f_s.at[j - 1], partner).wait_recv()
     load_go.wait()
     load_wo.wait()
-    out_gf = pltpu.make_async_copy(gfull, gf_o, st.at[4])
-    out_gf.start()
 
     def d_piece(n, carry):
         at = pl.ds(pl.multiple_of(n * half, half), half)
@@ -314,6 +385,28 @@
     lax.fori_loop(1, nctx, give, 0)
     dlr[ctx] = dls[ctx]
 
+    def out_weight(i, carry):
+        part = dot_tn(attn[...], gfull[:, strip_at(i)]).astype(BF)
+        there_y = lax.div(i, nx)
+        there_x = lax.rem(i, nx)
+        wos[0, there_x, there_y] = part[: cols // 2]
+        wos[1, there_y, there_x] = part[cols // 2 :]
+        return carry
+
+    lax.fori_loop(0, nctx, out_weight, 0)
+    out_wos = pltpu.make_async_copy(wos, wos_o, st.at[4])
+    out_wos.start()
+
+    for j in range(1, nx):
+        owner = lax.rem(x + j, nx)
+        for i in range(ny):
+            x_copy(j, i, owner).wait_recv()
+        pass_on(tx_o, owner, fx_s.at[j - 1], fx_r.at[j - 1]).start()
+    for j in range(1, ny):
+        owner = lax.rem(y + j, ny)
+        y_copy(j, owner).wait_recv()
+        pass_on(ty_o, owner, fy_s.at[j - 1], fy_r.at[j - 1]).start()
+
     def take(j, carry):
         source = lax.rem(ctx + j, nctx)
         copy = pltpu.make_async_remote_copy(
@@ -344,11 +437,38 @@
     out_dv.start()
     for send in first_sends + forwards:
         send.wait_send()
-    for copy in (out_attn, out_dq, out_dk, out_dv, out_gf):
+    for copy in [out_attn, out_dq, out_dk, out_dv, out_wos] + own_strips:
         copy.wait()
-
-
-def attention_core(nctx, ntp, tokens, w_query, w_key, w_value, w_out, block_doc, grad_out):
+    for j in range(1, nx):
+        for i in range(ny):
+            x_copy(j, i, x).wait_send()
+        passed = pass_on(tx_o, lax.rem(x + j, nx), fx_s.at[j - 1], fx_r.at[j - 1])
+        passed.wait_send()
+        other_half = pl.ds(pl.multiple_of((1 - core) * (rows // 2), rows // 2), rows // 2)
+        pltpu.make_async_remote_copy(
+            src_ref=tx_o.at[lax.rem(x + j, nx), other_half],
+            dst_ref=tx_o.at[lax.rem(x + j, nx), other_half],
+            send_sem=fx_s.at[j - 1],
+            recv_sem=fx_r.at[j - 1],
+            device_id={"tp": partner},
+            device_id_type=MESH,
+        ).wait_recv()
+    for j in range(1, ny):
+        y_copy(j, y).wait_send()
+        passed = pass_on(ty_o, lax.rem(y + j, ny), fy_s.at[j - 1], fy_r.at[j - 1])
+        passed.wait_send()
+        other_half = pl.ds(pl.multiple_of((1 - core) * (rows // 2), rows // 2), rows // 2)
+        pltpu.make_async_remote_copy(
+            src_ref=ty_o.at[lax.rem(y + j, ny), other_half],
+            dst_ref=ty_o.at[lax.rem(y + j, ny), other_half],
+            send_sem=fy_s.at[j - 1],
+            recv_sem=fy_r.at[j - 1],
+            device_id={"tp": partner},
+            device_id_type=MESH,
+        ).wait_recv()
+
+
+def attention_core(nctx, ntp, nx, tokens, w_query, w_key, w_value, w_out, block_doc, grad_out):
     rows, width = tokens.shape
     cols = w_query.shape[1]
     heads = cols // HDIM
@@ -356,14 +476,23 @@
     all_blocks = nctx * own_blocks
     per = 2 * own_blocks
     units = rows // PAIR * heads
+    ny = nctx // nx
     small = jax.ShapeDtypeStruct((rows, cols), BF)
     hbm = pl.BlockSpec(memory_space=pl.ANY)
     dma = pltpu.SemaphoreType.DMA
     return pl.pallas_call(
-        functools.partial(core_kernel, nctx, ntp),
-        out_shape=(small, small, small, small, jax.ShapeDtypeStruct((rows, width), BF)),
+        functools.partial(core_kernel, nctx, ntp, nx),
+        out_shape=(
+            small,
+            small,
+            small,
+            small,
+            jax.ShapeDtypeStruct((2, nx, ny, cols // 2, width // nctx), BF),
+            jax.ShapeDtypeStruct((nx, rows, width // nx), BF),
+            jax.ShapeDtypeStruct((ny, rows, width // ny), BF),
+        ),
         in_specs=[hbm] * 5 + [pl.BlockSpec(memory_space=pltpu.VMEM), hbm],
-        out_specs=(hbm,) * 5,
+        out_specs=(hbm,) * 7,
         scratch_shapes=[
             pltpu.VMEM((rows, width), BF),
             pltpu.VMEM((3, width, cols), BF),
@@ -385,6 +514,7 @@
             pltpu.VMEM((all_blocks, cols), F32),
             pltpu.VMEM((nctx, per, cols), BF),
             pltpu.VMEM((nctx, per, cols), BF),
+            pltpu.VMEM((2, nx, ny, cols // 2, width // nctx), BF),
             dma((6,)),
             dma((5,)),
             dma((ntp // 2,)),
@@ -394,6 +524,15 @@
             dma((nctx,)),
             dma((nctx - 1,)),
             dma((nctx,)),
+            dma((nx - 1, ny)),
+            dma((nx, ny)),
+            dma((ny - 1,)),
+            dma((ny,)),
+            dma((ny + 1,)),
+            dma((nx - 1,)),
+            dma((nx - 1,)),
+            dma((ny - 1,)),
+            dma((ny - 1,)),
         ],
         compiler_params=pltpu.CompilerParams(
             collective_id=1, has_side_effects=True, vmem_limit_bytes=64 * 1024 * 1024 - 65536
@@ -402,49 +541,498 @@
     )(tokens, w_query, w_key, w_value, w_out, block_doc.reshape(1, -1), grad_out)
 
 
-def cut_along(shard, dim, length):
-    dims = shard.shape
-    blocks = shard.reshape(*dims[:dim], length, dims[dim] // length, *dims[dim + 1 :])
-    return jnp.moveaxis(blocks, dim, 0)
-
-
-def sent_and_summed(shard, axis, dim):
-    length = lax.axis_size(axis)
-    blocks = lax.all_to_all(cut_along(shard, dim, length), axis, 0, 0, tiled=True)
-    return jnp.sum(blocks.astype(jnp.float32), axis=0)
-
-
-def per_device(nctx, ntp, tokens, w_query, w_key, w_value, w_out, block_doc, grad_out):
-    col_count = w_query.shape[1]
-    attn, d_query, d_key, d_value, upstream = attention_core(
-        nctx, ntp, tokens, w_query, w_key, w_value, w_out, block_doc, grad_out
+def grad_kernel(
+    nctx,
+    ntp,
+    nx,
+    dq_h,
+    dk_h,
+    dv_h,
+    attn_h,
+    wos_h,
+    tx_h,
+    ty_h,
+    wq_h,
+    wk_h,
+    wv_h,
+    wo_h,
+    tok_h,
+    go_h,
+    out_o,
+    gt_o,
+    gq_o,
+    gk_o,
+    gv_o,
+    gwo_o,
+    w3,
+    wo,
+    dcat,
+    attn,
+    rest,
+    rest_g,
+    gq,
+    gk,
+    gvx,
+    gvy,
+    o_p,
+    o_q,
+    o_z,
+    o_a,
+    d_p,
+    d_q,
+    d_z,
+    d_a,
+    sq,
+    sk,
+    sv,
+    rq,
+    rk,
+    rv,
+    oq,
+    ok,
+    ov,
+    wo_r,
+    wo_t,
+    wo_u,
+    wo_a,
+    ld,
+    ag_s,
+    ag_r,
+    op_s,
+    op_r,
+    oz_s,
+    oz_r,
+    dp_s,
+    dp_r,
+    dz_s,
+    dz_r,
+    rs_s,
+    rs_r,
+    w1_s,
+    w1_r,
+    w2_s,
+    w2_r,
+):
+    ctx = lax.axis_index("ctx")
+    tp = lax.axis_index("tp")
+    ny = nctx // nx
+    nz = ntp // 2
+    y = lax.div(ctx, nx)
+    x = lax.rem(ctx, nx)
+    core = lax.rem(tp, 2)
+    z = lax.div(tp, 2)
+    partner = tp + 1 - 2 * core
+    rows, cols = attn.shape
+    width = wo.shape[1]
+    strip = width // nctx
+    gathered = nx * rows
+    half = cols // 2
+
+    def block(t):
+        return pl.ds(pl.multiple_of(t * cols, cols), cols)
+
+    def strip_at(i):
+        return pl.ds(pl.multiple_of(i * strip, strip), strip)
+
+    def at_x(i):
+        return {"ctx": y * nx + i}
+
+    def at_y(i):
+        return {"ctx": i * nx + x}
+
+    def remote(source, target, send, recv, where):
+        return pltpu.make_async_remote_copy(
+            src_ref=source,
+            dst_ref=target,
+            send_sem=send,
+            recv_sem=recv,
+            device_id=where,
+            device_id_type=MESH,
+        )
+
+    loads = [
+        pltpu.make_async_copy(attn_h, attn, ld.at[0]),
+        pltpu.make_async_copy(wo_h, wo, ld.at[1]),
+    ]
+    for i, (d_h, w_h) in enumerate(((dq_h, wq_h), (dk_h, wk_h), (dv_h, wv_h))):
+        lanes = pl.ds(i * cols, cols)
+        loads.append(pltpu.make_async_copy(d_h, dcat.at[:, lanes], ld.at[2 + 2 * i]))
+        loads.append(pltpu.make_async_copy(w_h, w3.at[:, lanes], ld.at[3 + 2 * i]))
+    loads.append(pltpu.make_async_copy(tok_h.at[:, block(tp)], rest, ld.at[8]))
+    loads.append(pltpu.make_async_copy(go_h, rest_g, ld.at[9]))
+    lo = pl.ds(0, half)
+    hi = pl.ds(half, half)
+    gathers = (
+        (dq_h, gq, x, at_x, 0),
+        (dk_h, gk, y, at_y, 1),
+        (dv_h.at[:, lo], gvx, x, at_x, 2),
+        (dv_h.at[:, hi], gvy, y, at_y, 3),
     )
-    stacked = jnp.concatenate([d_query, d_key, d_value], axis=1)
-    joined = lax.psum_scatter(
-        dot_tn(tokens, stacked).astype(BF), "ctx", scatter_dimension=0, tiled=True
-    ).astype(F32)
-    grad_query_weight = joined[:, :col_count]
-    grad_key_weight = joined[:, col_count : 2 * col_count]
-    grad_value_weight = joined[:, 2 * col_count :]
-    summed = lax.psum_scatter(
-        dot_nn(attn, w_out).astype(BF), "tp", scatter_dimension=1, tiled=True
-    ).astype(F32)
-    shard_width = summed.shape[1]
-    residual = lax.dynamic_slice_in_dim(tokens, lax.axis_index("tp") * shard_width, shard_width, 1)
-    output = (residual.astype(F32) + summed).astype(BF)
-    d_partial = dot_nt(d_query, w_query) + dot_nt(d_key, w_key) + dot_nt(d_value, w_value)
-    d_summed = lax.psum_scatter(
-        d_partial.astype(BF), "tp", scatter_dimension=1, tiled=True
-    ).astype(F32)
-    grad_tokens = (grad_out.astype(F32) + d_summed).astype(BF)
-    grad_out_weight = sent_and_summed(dot_tn(attn, upstream).astype(BF), "ctx", 1)
-    return (
-        output,
-        grad_tokens,
-        grad_query_weight,
-        grad_key_weight,
-        grad_value_weight,
-        grad_out_weight,
+    for source, buf, pos, at, i in gathers:
+        loads.append(pltpu.make_async_copy(source, buf.at[pos], ld.at[10 + i]))
+    loads.append(pltpu.make_async_copy(wos_h.at[0, x], wo_r.at[0, x], ld.at[14]))
+    loads.append(pltpu.make_async_copy(wos_h.at[1, y], wo_r.at[1, y], ld.at[15]))
+    for load in loads:
+        load.start()
+
+    barrier = pltpu.get_barrier_semaphore()
+    for j in range(1, nx):
+        pl.semaphore_signal(
+            barrier, inc=1, device_id=at_x(lax.rem(x + j, nx)), device_id_type=MESH
+        )
+    for j in range(1, ny):
+        pl.semaphore_signal(
+            barrier, inc=1, device_id=at_y(lax.rem(y + j, ny)), device_id_type=MESH
+        )
+    for j in range(1, nz):
+        pl.semaphore_signal(
+            barrier,
+            inc=1,
+            device_id={"tp": lax.rem(z + j, nz) * 2 + core},
+            device_id_type=MESH,
+        )
+    pl.semaphore_signal(barrier, inc=1, device_id={"tp": partner}, device_id_type=MESH)
+    pl.semaphore_wait(barrier, nx + ny + nz - 2)
+
+    def near_send(gather, step):
+        source, buf, pos, at, i = gather
+        n = buf.shape[0]
+        there = lax.rem(pos + (1 if step == 0 else n - 1), n)
+        return remote(source, buf.at[pos], ag_s.at[i, step], ag_r.at[i, step], at(there))
+
+    def near_recv(gather, step):
+        source, buf, pos, at, i = gather
+        n = buf.shape[0]
+        owner = lax.rem(pos + (n - 1 if step == 0 else 1), n)
+        return remote(source, buf.at[owner], ag_s.at[i, step], ag_r.at[i, step], at(owner))
+
+    def relay(gather, step):
+        source, buf, pos, at, i = gather
+        n = buf.shape[0]
+        part = pl.ds(0, rows // 2) if step == 0 else pl.ds(rows // 2, rows // 2)
+        owner = lax.rem(pos + (n - 1 if step == 0 else 1), n)
+        there = lax.rem(pos + (1 if step == 0 else n - 1), n)
+        return remote(
+            buf.at[owner, part],
+            buf.at[owner, part],
+            ag_s.at[i, 2 + step],
+            ag_r.at[i, 2 + step],
+            at(there),
+        )
+
+    def relay_recv(gather, step):
+        source, buf, pos, at, i = gather
+        n = buf.shape[0]
+        part = pl.ds(0, rows // 2) if step == 0 else pl.ds(rows // 2, rows // 2)
+        owner = lax.rem(pos + 2, n)
+        return remote(
+            buf.at[owner, part],
+            buf.at[owner, part],
+            ag_s.at[i, 2 + step],
+            ag_r.at[i, 2 + step],
+            at(owner),
+        )
+
+    for gather in gathers:
+        near_send(gather, 0).start()
+        near_send(gather, 1).start()
+
+    def out_chunk(t):
+        return dot_nn(attn[...], wo[:, block(t)])
+
+    def tok_chunk(t):
+        return dot_nt(dcat[...], w3[block(t), :])
+
+    def to_partner(i, chunk, p, q, p_s, p_r):
+        return remote(p.at[i], q.at[i], p_s.at[i], p_r.at[i], {"tp": partner})
+
+    def summed_over_heads(chunk, p, q, zb, acc, p_s, p_r, z_s, z_r):
+        def first(i, carry):
+            p[i] = chunk(i * 2 + 1 - core).astype(BF)
+            to_partner(i, chunk, p, q, p_s, p_r).start()
+            return carry
+
+        lax.fori_loop(0, nz, first, 0)
+
+        def second(j, carry):
+            i = lax.rem(z + j, nz)
+            part = chunk(i * 2 + core)
+            copy = to_partner(i, chunk, p, q, p_s, p_r)
+            copy.wait_send()
+            copy.wait_recv()
+            part = part + q[i].astype(F32)
+
+            @pl.when(j < nz)
+            def _():
+                p[i] = part.astype(BF)
+                remote(
+                    p.at[i], zb.at[z], z_s.at[j - 1], z_r.at[z], {"tp": i * 2 + core}
+                ).start()
+
+            @pl.when(j == nz)
+            def _():
+                acc[...] = part
+
+            return carry
+
+        lax.fori_loop(1, nz + 1, second, 0)
+
+    def from_heads(p, zb, acc, z_s, z_r):
+        total = acc[...]
+        for j in range(1, nz):
+            i = lax.rem(z + j, nz)
+            copy = remote(p.at[i], zb.at[i], z_s.at[j - 1], z_r.at[i], {"tp": i * 2 + core})
+            copy.wait_send()
+            copy.wait_recv()
+            total = total + zb[i].astype(F32)
+        return total
+
+    loads[0].wait()
+    loads[1].wait()
+    summed_over_heads(out_chunk, o_p, o_q, o_z, o_a, op_s, op_r, oz_s, oz_r)
+    for load in loads[2:8]:
+        load.wait()
+    summed_over_heads(tok_chunk, d_p, d_q, d_z, d_a, dp_s, dp_r, dz_s, dz_r)
+    t_x = w3.at[pl.ds(0, gathered), pl.ds(0, width // nx)]
+    t_y = w3.at[pl.ds(gathered, gathered), pl.ds(0, width // ny)]
+    late = []
+    for i in range(nx):
+        part = pl.ds(i * rows, rows)
+        late.append(pltpu.make_async_copy(tx_h.at[i], t_x.at[part], ld.at[16 + i]))
+        late.append(pltpu.make_async_copy(ty_h.at[i], t_y.at[part], ld.at[16 + nx + i]))
+    for load in late:
+        load.start()
+
+    for gather in gathers:
+        for step in range(2):
+            near_recv(gather, step).wait_recv()
+            relay(gather, step).start()
+
+    def first_hop(j, side, owner):
+        pos, n, at = ((x, nx, at_x), (y, ny, at_y))[side]
+        there = lax.rem(pos + j, n)
+        return remote(
+            wos_h.at[side, there],
+            wo_r.at[side, owner],
+            w1_s.at[side, j - 1],
+            w1_r.at[side, owner],
+            at(there),
+        )
+
+    for j in (1, 3, 2):
+        first_hop(j, 0, x).start()
+        first_hop(j, 1, y).start()
+
+    for load in loads[8:] + late:
+        load.wait()
+
+    sends = (
+        (gathers[0], 0, sq, rq, oq, y, at_y, 0),
+        (gathers[1], 1, sk, rk, ok, x, at_x, 1),
+        (gathers[2], 0, sv.at[:, :, lo], rv.at[:, :, lo], ov.at[:, lo], y, at_y, 2),
+        (gathers[3], 1, sv.at[:, :, hi], rv.at[:, :, hi], ov.at[:, hi], x, at_x, 3),
+    )
+
+    def weight_send(item, there, slot, owner):
+        gather, side, s, r, o, pos, at, i = item
+        return remote(s.at[there], r.at[owner], rs_s.at[i, slot], rs_r.at[i, owner], at(there))
+
+    for item in sends:
+        gather, side, s, r, o, pos, at, i = item
+        for step in range(2):
+            relay_recv(gather, step).wait_recv()
+        buf = gather[1]
+        n = buf.shape[0]
+        base = pl.ds(side * gathered, gathered)
+
+        def weight_piece(j, carry):
+            there = lax.rem(pos + j, n)
+            part = dot_tn(
+                w3[base, strip_at(there)], buf[...].reshape(gathered, buf.shape[2])
+            )
+
+            @pl.when(j < n)
+            def _():
+                s[there] = part.astype(BF)
+                weight_send(item, there, j - 1, pos).start()
+
+            @pl.when(j == n)
+            def _():
+                o[...] = part
+
+            return carry
+
+        lax.fori_loop(1, n + 1, weight_piece, 0)
+
+    out_o[...] = (rest[...].astype(F32) + from_heads(o_p, o_z, o_a, oz_s, oz_r)).astype(BF)
+    gt_o[...] = (rest_g[...].astype(F32) + from_heads(d_p, d_z, d_a, dz_s, dz_r)).astype(BF)
+
+    def second_hop(side, there, slot, owner):
+        pos, n, at = ((y, ny, at_y), (x, nx, at_x))[side]
+        return remote(
+            wo_t.at[side, there],
+            wo_u.at[side, owner],
+            w2_s.at[side, slot],
+            w2_r.at[side, owner],
+            at(there),
+        )
+
+    for side in range(2):
+        here, n = ((x, nx), (y, ny))[side]
+        pos, m = ((y, ny), (x, nx))[side]
+        for j in range(1, n):
+            copy = first_hop(j, side, lax.rem(here + j, n))
+            copy.wait_send()
+            copy.wait_recv()
+
+        def add_up(j, carry):
+            there = lax.rem(pos + j, m)
+            total = wo_r[side, 0, there].astype(F32)
+            for k in range(1, n):
+                total = total + wo_r[side, k, there].astype(F32)
+
+            @pl.when(j < m)
+            def _():
+                wo_t[side, there] = total.astype(BF)
+                second_hop(side, there, j - 1, pos).start()
+
+            @pl.when(j == m)
+            def _():
+                wo_a[pl.ds(side * half, half), :] = total
+
+            return carry
+
+        lax.fori_loop(1, m + 1, add_up, 0)
+
+    for item, target in zip(sends, (gq_o, gk_o, gv_o.at[:, lo], gv_o.at[:, hi])):
+        gather, side, s, r, o, pos, at, i = item
+        n = r.shape[0]
+        total = o[...]
+        for j in range(1, n):
+            there = lax.rem(pos + j, n)
+            copy = weight_send(item, there, j - 1, there)
+            copy.wait_send()
+            copy.wait_recv()
+            total = total + r[there].astype(F32)
+        target[...] = total
+        for step in range(2):
+            near_send(gather, step).wait_send()
+            relay(gather, step).wait_send()
+
+    for side in range(2):
+        pos, m = ((y, ny), (x, nx))[side]
+        total = wo_a[pl.ds(side * half, half), :]
+        for j in range(1, m):
+            there = lax.rem(pos + j, m)
+            copy = second_hop(side, there, j - 1, there)
+            copy.wait_send()
+            copy.wait_recv()
+            total = total + wo_u[side, there].astype(F32)
+        gwo_o[pl.ds(side * half, half), :] = total
+
+
+def gradients(nctx, ntp, nx, core_out, tokens, w_query, w_key, w_value, w_out, grad_out):
+    attn, d_query, d_key, d_value, wos, tx, ty = core_out
+    rows, width = tokens.shape
+    cols = w_query.shape[1]
+    ny = nctx // nx
+    nz = ntp // 2
+    strip = width // nctx
+    half = cols // 2
+    hbm = pl.BlockSpec(memory_space=pl.ANY)
+    vmem = pl.BlockSpec(memory_space=pltpu.VMEM)
+    dma = pltpu.SemaphoreType.DMA
+    small = jax.ShapeDtypeStruct((rows, cols), BF)
+    piece = jax.ShapeDtypeStruct((strip, cols), F32)
+    heads_scratch = [
+        pltpu.VMEM((nz, rows, cols), BF),
+        pltpu.VMEM((nz, rows, cols), BF),
+        pltpu.VMEM((nz, rows, cols), BF),
+        pltpu.VMEM((rows, cols), F32),
+    ]
+    return pl.pallas_call(
+        functools.partial(grad_kernel, nctx, ntp, nx),
+        out_shape=(
+            small,
+            small,
+            piece,
+            piece,
+            piece,
+            jax.ShapeDtypeStruct((cols, strip), F32),
+        ),
+        in_specs=[hbm] * 13,
+        out_specs=(vmem,) * 6,
+        scratch_shapes=[
+            pltpu.VMEM((width, 3 * cols), BF),
+            pltpu.VMEM((cols, width), BF),
+            pltpu.VMEM((rows, 3 * cols), BF),
+            pltpu.VMEM((rows, cols), BF),
+            pltpu.VMEM((rows, cols), BF),
+            pltpu.VMEM((rows, cols), BF),
+            pltpu.VMEM((nx, rows, cols), BF),
+            pltpu.VMEM((ny, rows, cols), BF),
+            pltpu.VMEM((nx, rows, half), BF),
+            pltpu.VMEM((ny, rows, half), BF),
+            *heads_scratch,
+            *heads_scratch,
+            pltpu.VMEM((ny, strip, cols), BF),
+            pltpu.VMEM((nx, strip, cols), BF),
+            pltpu.VMEM((ny, strip, cols), BF),
+            pltpu.VMEM((ny, strip, cols), BF),
+            pltpu.VMEM((nx, strip, cols), BF),
+            pltpu.VMEM((ny, strip, cols), BF),
+            pltpu.VMEM((strip, cols), F32),
+            pltpu.VMEM((strip, cols), F32),
+            pltpu.VMEM((strip, cols), F32),
+            pltpu.VMEM((2, nx, ny, half, strip), BF),
+            pltpu.VMEM((2, ny, half, strip), BF),
+            pltpu.VMEM((2, ny, half, strip), BF),
+            pltpu.VMEM((cols, strip), F32),
+            dma((16 + nx + ny,)),
+            dma((4, 4)),
+            dma((4, 4)),
+            dma((nz,)),
+            dma((nz,)),
+            dma((nz - 1,)),
+            dma((nz,)),
+            dma((nz,)),
+            dma((nz,)),
+            dma((nz - 1,)),
+            dma((nz,)),
+            dma((4, nx - 1)),
+            dma((4, nx)),
+            dma((2, nx - 1)),
+            dma((2, nx)),
+            dma((2, nx - 1)),
+            dma((2, nx)),
+        ],
+        compiler_params=pltpu.CompilerParams(
+            collective_id=2, has_side_effects=True, vmem_limit_bytes=64 * 1024 * 1024 - 65536
+        ),
+        name="gradients",
+    )(
+        d_query,
+        d_key,
+        d_value,
+        attn,
+        wos,
+        tx,
+        ty,
+        w_query,
+        w_key,
+        w_value,
+        w_out,
+        tokens,
+        grad_out,
+    )
+
+
+def per_device(nctx, ntp, nx, tokens, w_query, w_key, w_value, w_out, block_doc, grad_out):
+    core_out = attention_core(
+        nctx, ntp, nx, tokens, w_query, w_key, w_value, w_out, block_doc, grad_out
+    )
+    return tuple(
+        gradients(nctx, ntp, nx, core_out, tokens, w_query, w_key, w_value, w_out, grad_out)
     )
 
 
@@ -467,7 +1055,7 @@
         P("tp", "ctx"),
     )
     return jax.shard_map(
-        functools.partial(per_device, mesh.shape["ctx"], mesh.shape["tp"]),
+        functools.partial(per_device, mesh.shape["ctx"], mesh.shape["tp"], math.isqrt(mesh.shape["ctx"])),
         mesh=mesh,
         in_specs=in_specs,
         out_specs=out_specs,

time: 262 us -> 145 us (0.55)
  waiting for transfers between devices: 134 us -> 0 us
  Pallas kernels: 50.2 us -> 135 us
  matrix products: 41.6 us -> 0 us
  between operations: 13.8 us -> 0.67 us
  other arithmetic: 7.77 us -> 0 us
  starting transfers between devices: 5.76 us -> 0 us
    pallas_call x1 -> x2, Pallas kernels: 50.2 us -> 135 us  [the longest x1 77.3 us: gradients(): pl.pallas_call(functools.partial(grad_kernel, nctx, ntp, nx), out_shape=(...]
    all_to_all x1 -> x0, waiting for transfers between devices: 74.3 us -> none  [sent_and_summed(): lax.all_to_all(cut_along(shard, dim, length), axis, 0, 0, tiled=True)]
    reduce_scatter x3 -> x0, waiting for transfers between devices: 59.6 us -> none  [the longest x1 59.6 us: per_device(): lax.psum_scatter(dot_tn(tokens, stacked).astype(BF), 'ctx', scatter_dimen...]
    dot_general x6 -> x0, matrix products: 41.6 us -> none  [the longest x3 18.3 us: dot_nt(): lax.dot_general(a, b, (((1,), (1,)), ((), ())), preferred_element_type=F32)]
    all_to_all x1 -> x0, starting transfers between devices: 5.46 us -> none  [sent_and_summed(): lax.all_to_all(cut_along(shard, dim, length), axis, 0, 0, tiled=True)]
    unnamed x17 -> x10, local copies, waits for them, and re-layouts: 5 us -> 9.15 us
    convert_element_type x2 -> x0, other arithmetic: 4.11 us -> none  [the longest x1 2.13 us: per_device(): output = (residual.astype(F32) + summed).astype(BF)]
    reduce_sum x1 -> x0, other arithmetic: 3.66 us -> none  [sent_and_summed(): return jnp.sum(blocks.astype(jnp.float32), axis=0)]
  transfers between devices with their start and end apart: 4 -> 0, of which waited for: 2 -> 0; matrix products, arithmetic and copies ran while one was open for 17% -> 0% of each run, Pallas kernels for 0% -> 0%
where the time goes in v3:
time: 145 us; the launch traced here: 144 us
  Pallas kernels  135 us (93%)
  local copies, waits for them, and re-layouts  9.15 us (6%)
    pallas_call x1, Pallas kernels, gradients(): pl.pallas_call(functools.partial(grad_kernel, nctx, ntp, nx), out_shape=(...  77.3 us
    pallas_call x1, Pallas kernels, attention_core(): pl.pallas_call(functools.partial(core_kernel, nctx, ntp, nx), out_shape=(...  57.2 us
    unnamed x10, local copies, waits for them, and re-layouts  9.15 us

profile of v3, /device:TPU:1, one launch (start us, length us, event | category | flops | bytes accessed | tf_op | source)
XLA Modules:
  0.0 144.3 jit_solution(8474480980410927471)
XLA Ops:
  0.6 57.2 %attention_core.1 = (bf16[512,512]{1,0:T(8,128)(2,1)}, bf16[512,512]{1,0:T(8,128)(2,1)}, bf16[512,512]{1,0:T(8,128)(2,1)}, bf16[512,512]{1,0:T(8,128)(2,1)}, bf1...) custom-call(bf16[512,4096]{1,0:T(8,128)(2,1)} %tok_h.3, ...), custom_call_target="tpu_custom_call" | custom-call | tf_op jit(solution)/shard_map/attention_core/pallas_call | solution.py:483
  57.8 77.3 %gradients.1 = (bf16[512,512]{1,0:T(8,128)(2,1)}, bf16[512,512]{1,0:T(8,128)(2,1)}, f32[256,512]{1,0:T(8,128)}, f32[256,512]{1,0:T(8,128)}, f32[256,512]{1,0:T(8,128)}, /*index=5*/f32[512,256]{1,0:T(8,128)}) custom-call(bf16[512,512]{1,0:T(8,128)(2,1)} %get-tuple-element.13.dq_h, bf16[512,512]{1,0:T(8,128)(2,1)} %get-tuple-element.14.dk_h, ...), custom_call_target="tpu_custom_call" | custom-call | tf_op jit(solution)/shard_map/gradients/pallas_call | solution.py:953
  135.2 0.0 copy-start.1
  135.2 0.0 copy-start
  135.2 2.0 %copy.19 = bf16[512,512]{1,0:T(8,128)(2,1)} copy(bf16[512,512]{1,0:T(8,128)(2,1)} %get-tuple-element.26) | data formatting | bytes 1048576
  137.1 1.9 %copy.20 = bf16[512,512]{1,0:T(8,128)(2,1)} copy(bf16[512,512]{1,0:T(8,128)(2,1)} %get-tuple-element.27) | data formatting | bytes 1048576
  139.0 1.9 %copy.21 = f32[256,512]{1,0:T(8,128)} copy(f32[256,512]{1,0:T(8,128)} %get-tuple-element.28) | data formatting | bytes 1048576
  140.9 1.9 %copy.22 = f32[256,512]{1,0:T(8,128)} copy(f32[256,512]{1,0:T(8,128)} %get-tuple-element.29) | data formatting | bytes 1048576
  142.7 0.0 copy-done.1
  142.7 0.8 copy.23
  143.5 0.0 copy-done
  143.5 0.8 copy.24
Async XLA Ops:
  135.2 7.6 %copy-start.1 = (f32[256,512]{1,0:T(8,128)S(1)}, f32[256,512]{1,0:T(8,128)}, u32[]{:S(2)}) copy-start(f32[256,512]{1,0:T(8,128)} %get-tuple-element.30) | copy-start | bytes 1572868
  135.2 8.4 %copy-start = (f32[512,256]{1,0:T(8,128)S(1)}, f32[512,256]{1,0:T(8,128)}, u32[]{:S(2)}) copy-start(f32[512,256]{1,0:T(8,128)} %get-tuple-element.31) | copy-start | bytes 1572868

commit v4 on v3

--- a/solution.py
+++ b/solution.py
@@ -591,6 +591,9 @@
     oq,
     ok,
     ov,
+    wo_own,
+    wo_nb,
+    wo_far,
     wo_r,
     wo_t,
     wo_u,
@@ -606,8 +609,12 @@
     dp_r,
     dz_s,
     dz_r,
+    rf_s,
+    rf_r,
     rs_s,
     rs_r,
+    w0_s,
+    w0_r,
     w1_s,
     w1_r,
     w2_s,
@@ -670,8 +677,17 @@
     )
     for source, buf, pos, at, i in gathers:
         loads.append(pltpu.make_async_copy(source, buf.at[pos], ld.at[10 + i]))
-    loads.append(pltpu.make_async_copy(wos_h.at[0, x], wo_r.at[0, x], ld.at[14]))
-    loads.append(pltpu.make_async_copy(wos_h.at[1, y], wo_r.at[1, y], ld.at[15]))
+    rings = ((x, nx, at_x), (y, ny, at_y))
+    for side in range(2):
+        pos, n, at = rings[side]
+        for k, target in ((0, wo_own), (1, wo_nb.at[:, 0]), (n - 1, wo_nb.at[:, 1])):
+            loads.append(
+                pltpu.make_async_copy(
+                    wos_h.at[side, lax.rem(pos + k, n)],
+                    target.at[side],
+                    ld.at[14 + 3 * side + min(k, 2)],
+                )
+            )
     for load in loads:
         load.start()
 
@@ -737,6 +753,33 @@
         near_send(gather, 0).start()
         near_send(gather, 1).start()
 
+    subs = (pl.ds(0, nx // 2), pl.ds(nx // 2, nx // 2))
+
+    def far_hop(side, way):
+        pos, n, at = rings[side]
+        return remote(
+            wos_h.at[side, lax.rem(pos + 2, n), subs[way]],
+            wo_far.at[side, subs[way]],
+            w0_s.at[side, way],
+            w0_r.at[side, way],
+            at(lax.rem(pos + (1 if way == 0 else n - 1), n)),
+        )
+
+    def near_hop(side, way, added):
+        pos, n, at = rings[side]
+        part = subs[way if added else 1 - way]
+        return remote(
+            wo_nb.at[side, way, part],
+            wo_r.at[side, way, part],
+            w1_s.at[side, way, 1 if added else 0],
+            w1_r.at[side, way, 1 if added else 0],
+            at(lax.rem(pos + (1 if way == 0 else n - 1), n)),
+        )
+
+    for way in range(2):
+        for side in range(2):
+            far_hop(side, way).start()
+
     def out_chunk(t):
         return dot_nn(attn[...], wo[:, block(t)])
 
@@ -798,8 +841,8 @@
     late = []
     for i in range(nx):
         part = pl.ds(i * rows, rows)
-        late.append(pltpu.make_async_copy(tx_h.at[i], t_x.at[part], ld.at[16 + i]))
-        late.append(pltpu.make_async_copy(ty_h.at[i], t_y.at[part], ld.at[16 + nx + i]))
+        late.append(pltpu.make_async_copy(tx_h.at[i], t_x.at[part], ld.at[20 + i]))
+        late.append(pltpu.make_async_copy(ty_h.at[i], t_y.at[part], ld.at[20 + nx + i]))
     for load in late:
         load.start()
 
@@ -808,23 +851,20 @@
             near_recv(gather, step).wait_recv()
             relay(gather, step).start()
 
-    def first_hop(j, side, owner):
-        pos, n, at = ((x, nx, at_x), (y, ny, at_y))[side]
-        there = lax.rem(pos + j, n)
-        return remote(
-            wos_h.at[side, there],
-            wo_r.at[side, owner],
-            w1_s.at[side, j - 1],
-            w1_r.at[side, owner],
-            at(there),
-        )
-
-    for j in (1, 3, 2):
-        first_hop(j, 0, x).start()
-        first_hop(j, 1, y).start()
-
     for load in loads[8:] + late:
         load.wait()
+
+    for side in range(2):
+        for way in range(2):
+            near_hop(side, way, False).start()
+    for side in range(2):
+        for way in range(2):
+            far_hop(side, way).wait_recv()
+            part = subs[way]
+            wo_nb[side, way, part] = (
+                wo_nb[side, way, part].astype(F32) + wo_far[side, part].astype(F32)
+            ).astype(BF)
+            near_hop(side, way, True).start()
 
     sends = (
         (gathers[0], 0, sq, rq, oq, y, at_y, 0),
@@ -832,10 +872,30 @@
         (gathers[2], 0, sv.at[:, :, lo], rv.at[:, :, lo], ov.at[:, lo], y, at_y, 2),
         (gathers[3], 1, sv.at[:, :, hi], rv.at[:, :, hi], ov.at[:, hi], x, at_x, 3),
     )
-
-    def weight_send(item, there, slot, owner):
+    ends = (pl.ds(0, strip // 2), pl.ds(strip // 2, strip // 2))
+
+    def weight_far(item, way):
         gather, side, s, r, o, pos, at, i = item
-        return remote(s.at[there], r.at[owner], rs_s.at[i, slot], rs_r.at[i, owner], at(there))
+        n = nx
+        return remote(
+            s.at[0, ends[way]],
+            r.at[0, ends[way]],
+            rf_s.at[i, way],
+            rf_r.at[i, way],
+            at(lax.rem(pos + (1 if way == 0 else n - 1), n)),
+        )
+
+    def weight_near(item, way, added):
+        gather, side, s, r, o, pos, at, i = item
+        n = nx
+        part = ends[way if added else 1 - way]
+        return remote(
+            s.at[1 + way, part],
+            r.at[1 + way, part],
+            rs_s.at[i, way, 1 if added else 0],
+            rs_r.at[i, way, 1 if added else 0],
+            at(lax.rem(pos + (1 if way == 0 else n - 1), n)),
+        )
 
     for item in sends:
         gather, side, s, r, o, pos, at, i = item
@@ -845,24 +905,45 @@
         n = buf.shape[0]
         base = pl.ds(side * gathered, gathered)
 
-        def weight_piece(j, carry):
-            there = lax.rem(pos + j, n)
+        def weight_piece(k, carry):
+            there = lax.rem(pos + 6 - k, n)
             part = dot_tn(
                 w3[base, strip_at(there)], buf[...].reshape(gathered, buf.shape[2])
             )
 
-            @pl.when(j < n)
+            @pl.when(k == 0)
             def _():
-                s[there] = part.astype(BF)
-                weight_send(item, there, j - 1, pos).start()
-
-            @pl.when(j == n)
+                s[0] = part.astype(BF)
+                weight_far(item, 0).start()
+                weight_far(item, 1).start()
+
+            @pl.when(k == 1)
+            def _():
+                s[1] = part.astype(BF)
+                weight_near(item, 0, False).start()
+
+            @pl.when(k == 2)
             def _():
                 o[...] = part
 
+            @pl.when(k == 3)
+            def _():
+                s[2] = part.astype(BF)
+                weight_near(item, 1, False).start()
+
             return carry
 
-        lax.fori_loop(1, n + 1, weight_piece, 0)
+        lax.fori_loop(0, n, weight_piece, 0)
+
+    for item in sends:
+        gather, side, s, r, o, pos, at, i = item
+        for way in range(2):
+            weight_far(item, way).wait_recv()
+            part = ends[way]
+            s[1 + way, part] = (
+                s[1 + way, part].astype(F32) + r[0, part].astype(F32)
+            ).astype(BF)
+            weight_near(item, way, True).start()
 
     out_o[...] = (rest[...].astype(F32) + from_heads(o_p, o_z, o_a, oz_s, oz_r)).astype(BF)
     gt_o[...] = (rest_g[...].astype(F32) + from_heads(d_p, d_z, d_a, dz_s, dz_r)).astype(BF)
@@ -878,18 +959,19 @@
         )
 
     for side in range(2):
-        here, n = ((x, nx), (y, ny))[side]
         pos, m = ((y, ny), (x, nx))[side]
-        for j in range(1, n):
-            copy = first_hop(j, side, lax.rem(here + j, n))
-            copy.wait_send()
-            copy.wait_recv()
+        for way in range(2):
+            far_hop(side, way).wait_send()
+            for added in (False, True):
+                copy = near_hop(side, way, added)
+                copy.wait_send()
+                copy.wait_recv()
 
         def add_up(j, carry):
             there = lax.rem(pos + j, m)
-            total = wo_r[side, 0, there].astype(F32)
-            for k in range(1, n):
-                total = total + wo_r[side, k, there].astype(F32)
+            total = wo_own[side, there].astype(F32)
+            for way in range(2):
+                total = total + wo_r[side, way, there].astype(F32)
 
             @pl.when(j < m)
             def _():
@@ -906,15 +988,13 @@
 
     for item, target in zip(sends, (gq_o, gk_o, gv_o.at[:, lo], gv_o.at[:, hi])):
         gather, side, s, r, o, pos, at, i = item
-        n = r.shape[0]
-        total = o[...]
-        for j in range(1, n):
-            there = lax.rem(pos + j, n)
-            copy = weight_send(item, there, j - 1, there)
-            copy.wait_send()
-            copy.wait_recv()
-            total = total + r[there].astype(F32)
-        target[...] = total
+        for way in range(2):
+            weight_far(item, way).wait_send()
+            for added in (False, True):
+                copy = weight_near(item, way, added)
+                copy.wait_send()
+                copy.wait_recv()
+        target[...] = o[...] + r[1].astype(F32) + r[2].astype(F32)
         for step in range(2):
             near_send(gather, step).wait_send()
             relay(gather, step).wait_send()
@@ -975,20 +1055,23 @@
             pltpu.VMEM((ny, rows, half), BF),
             *heads_scratch,
             *heads_scratch,
-            pltpu.VMEM((ny, strip, cols), BF),
-            pltpu.VMEM((nx, strip, cols), BF),
-            pltpu.VMEM((ny, strip, cols), BF),
-            pltpu.VMEM((ny, strip, cols), BF),
-            pltpu.VMEM((nx, strip, cols), BF),
-            pltpu.VMEM((ny, strip, cols), BF),
+            pltpu.VMEM((3, strip, cols), BF),
+            pltpu.VMEM((3, strip, cols), BF),
+            pltpu.VMEM((3, strip, cols), BF),
+            pltpu.VMEM((3, strip, cols), BF),
+            pltpu.VMEM((3, strip, cols), BF),
+            pltpu.VMEM((3, strip, cols), BF),
             pltpu.VMEM((strip, cols), F32),
             pltpu.VMEM((strip, cols), F32),
             pltpu.VMEM((strip, cols), F32),
-            pltpu.VMEM((2, nx, ny, half, strip), BF),
+            pltpu.VMEM((2, ny, half, strip), BF),
+            pltpu.VMEM((2, 2, ny, half, strip), BF),
+            pltpu.VMEM((2, ny, half, strip), BF),
+            pltpu.VMEM((2, 2, ny, half, strip), BF),
             pltpu.VMEM((2, ny, half, strip), BF),
             pltpu.VMEM((2, ny, half, strip), BF),
             pltpu.VMEM((cols, strip), F32),
-            dma((16 + nx + ny,)),
+            dma((20 + nx + ny,)),
             dma((4, 4)),
             dma((4, 4)),
             dma((nz,)),
@@ -999,10 +1082,14 @@
             dma((nz,)),
             dma((nz - 1,)),
             dma((nz,)),
-            dma((4, nx - 1)),
-            dma((4, nx)),
-            dma((2, nx - 1)),
-            dma((2, nx)),
+            dma((4, 2)),
+            dma((4, 2)),
+            dma((4, 2, 2)),
+            dma((4, 2, 2)),
+            dma((2, 2)),
+            dma((2, 2)),
+            dma((2, 2, 2)),
+            dma((2, 2, 2)),
             dma((2, nx - 1)),
             dma((2, nx)),
         ],
@@ -1027,11 +1114,40 @@
     )
 
 
+def settle_kernel(count, *refs):
+    ins, outs, bufs = refs[:count], refs[count : 2 * count], refs[2 * count : 3 * count]
+    come, go = refs[3 * count :]
+    first = [pltpu.make_async_copy(ins[i], bufs[i], come.at[i]) for i in range(count)]
+    second = [pltpu.make_async_copy(bufs[i], outs[i], go.at[i]) for i in range(count)]
+    for copy in first:
+        copy.start()
+    for i in range(count):
+        first[i].wait()
+        second[i].start()
+    for copy in second:
+        copy.wait()
+
+
+def settled(arrays):
+    count = len(arrays)
+    hbm = pl.BlockSpec(memory_space=pl.ANY)
+    shapes = [(a.shape, a.dtype) for a in arrays]
+    return pl.pallas_call(
+        functools.partial(settle_kernel, count),
+        out_shape=tuple(jax.ShapeDtypeStruct(*s) for s in shapes),
+        in_specs=[hbm] * count,
+        out_specs=(hbm,) * count,
+        scratch_shapes=[pltpu.VMEM(*s) for s in shapes]
+        + [pltpu.SemaphoreType.DMA((count,)), pltpu.SemaphoreType.DMA((count,))],
+        name="settled",
+    )(*arrays)
+
+
 def per_device(nctx, ntp, nx, tokens, w_query, w_key, w_value, w_out, block_doc, grad_out):
     core_out = attention_core(
         nctx, ntp, nx, tokens, w_query, w_key, w_value, w_out, block_doc, grad_out
     )
-    return tuple(
+    return settled(
         gradients(nctx, ntp, nx, core_out, tokens, w_query, w_key, w_value, w_out, grad_out)
     )
 

time: 145 us -> 128 us (0.88)
  local copies, waits for them, and re-layouts: 9.15 us -> 0 us
  Pallas kernels: 135 us -> 128 us
    pallas_call x1, Pallas kernels: 77.3 us -> 67.7 us  [gradients(): pl.pallas_call(functools.partial(grad_kernel, nctx, ntp, nx), out_shape=(...]
    unnamed x10 -> x0, local copies, waits for them, and re-layouts: 9.15 us -> none
    pallas_call x0 -> x1, Pallas kernels: none -> 2.8 us  [settled(): pl.pallas_call(functools.partial(settle_kernel, count), out_shape=tuple((...]
where the time goes in v4:
time: 128 us
  Pallas kernels  128 us (100%)
    pallas_call x1, Pallas kernels, gradients(): pl.pallas_call(functools.partial(grad_kernel, nctx, ntp, nx), out_shape=(...  67.7 us
    pallas_call x1, Pallas kernels, attention_core(): pl.pallas_call(functools.partial(core_kernel, nctx, ntp, nx), out_shape=(...  57.2 us
    pallas_call x1, Pallas kernels, settled(): pl.pallas_call(functools.partial(settle_kernel, count), out_shape=tuple((...  2.8 us

profile of v4, /device:TPU:1, one launch (start us, length us, event | category | flops | bytes accessed | tf_op | source)
XLA Modules:
  0.0 128.3 jit_solution(4617186656475730304)
XLA Ops:
  0.6 57.2 %attention_core.1 = (bf16[512,512]{1,0:T(8,128)(2,1)}, bf16[512,512]{1,0:T(8,128)(2,1)}, bf16[512,512]{1,0:T(8,128)(2,1)}, bf16[512,512]{1,0:T(8,128)(2,1)}, bf1...) custom-call(bf16[512,4096]{1,0:T(8,128)(2,1)} %tok_h.3, ...), custom_call_target="tpu_custom_call" | custom-call | tf_op jit(solution)/shard_map/attention_core/pallas_call | solution.py:483
  57.8 67.7 %gradients.1 = (bf16[512,512]{1,0:T(8,128)(2,1)}, bf16[512,512]{1,0:T(8,128)(2,1)}, f32[256,512]{1,0:T(8,128)}, f32[256,512]{1,0:T(8,128)}, f32[256,512]{1,0:T(8,128)}, /*index=5*/f32[512,256]{1,0:T(8,128)}) custom-call(bf16[512,512]{1,0:T(8,128)(2,1)} %get-tuple-element.19.dq_h, bf16[512,512]{1,0:T(8,128)(2,1)} %get-tuple-element.20.dk_h, ...), custom_call_target="tpu_custom_call" | custom-call | tf_op jit(solution)/shard_map/gradients/pallas_call | solution.py:1033
  125.5 2.8 %settled.1 = (bf16[512,512]{1,0:T(8,128)(2,1)}, bf16[512,512]{1,0:T(8,128)(2,1)}, f32[256,512]{1,0:T(8,128)}, f32[256,512]{1,0:T(8,128)}, f32[256,512]{1,0:T(8,128)}, /*index=5*/f32[512,256]{1,0:T(8,128)}) custom-call(bf16[512,512]{1,0:T(8,128)(2,1)} %get-tuple-element.26.refs_0_, bf16[512,512]{1,0:T(8,128)(2,1)} %get-tuple-element.27.refs_1_, ...), custom_call_target="tpu_custom_call" | custom-call | tf_op jit(solution)/shard_map/settled/pallas_call | solution.py:1135

commit v5 on v4

--- a/solution.py
+++ b/solution.py
@@ -76,6 +76,7 @@
     dls,
     dlr,
     wos,
+    acc,
     ld,
     st,
     g_s,
@@ -94,6 +95,8 @@
     fx_r,
     fy_s,
     fy_r,
+    h_s,
+    h_r,
 ):
     ctx = lax.axis_index("ctx")
     ny = nctx // nx
@@ -151,8 +154,11 @@
             device_id_type=MESH,
         )
 
-    first_sends = [grad_copy(go_h, tp, g_s.at[j - 1], mate(j, core)) for j in range(1, nz)]
-    first_sends.append(grad_copy(go_h, tp, g_s.at[nz - 1], partner))
+    first_sends = [
+        grad_copy(go_h, tp, g_s.at[0], mate(1, core)),
+        grad_copy(go_h, tp, g_s.at[1], mate(nz - 1, core)),
+        grad_copy(go_h, tp, g_s.at[2], partner),
+    ]
     for send in first_sends:
         send.start()
 
@@ -211,7 +217,46 @@
         copy.wait_recv()
         return carry
 
+    def row_half(way):
+        return pl.ds(way * (rows // 2), rows // 2)
+
+    def relay(way):
+        owner = mate(nz - 1 if way == 0 else 1, core)
+        view = gfull.at[row_half(way), shard(owner)]
+        return pltpu.make_async_remote_copy(
+            src_ref=view,
+            dst_ref=view,
+            send_sem=h_s.at[way],
+            recv_sem=h_r.at[way],
+            device_id={"tp": mate(1 if way == 0 else nz - 1, core)},
+            device_id_type=MESH,
+        )
+
+    def relay_wait(way):
+        view = gfull.at[row_half(way), shard(mate(2, core))]
+        pltpu.make_async_remote_copy(
+            src_ref=view,
+            dst_ref=view,
+            send_sem=h_s.at[way],
+            recv_sem=h_r.at[way],
+            device_id={"tp": mate(nz - 1 if way == 0 else 1, core)},
+            device_id_type=MESH,
+        ).wait_recv()
+
     lax.fori_loop(1, nctx, land_wait, 0)
+
+    forwards = []
+
+    def pass_shard(owner, slot):
+        onward = grad_copy(gfull.at[:, shard(owner)], owner, f_s.at[slot], partner)
+        onward.start()
+        forwards.append(onward)
+
+    for way in range(2):
+        owner = mate(nz - 1 if way == 0 else 1, core)
+        grad_copy(gfull.at[:, shard(owner)], owner, f_s.at[way], partner).wait_recv()
+        relay(way).start()
+        pass_shard(owner, way)
 
     strip = width // nctx
     own_half = pl.ds(pl.multiple_of(core * (rows // 2), rows // 2), rows // 2)
@@ -312,26 +357,52 @@
     out_attn = pltpu.make_async_copy(attn, attn_o, st.at[0])
     out_attn.start()
 
-    forwards = []
-    for j in range(1, nz):
-        owner = mate(j, core)
-        grad_copy(gfull.at[:, shard(owner)], owner, f_s.at[j - 1], partner).wait_recv()
-        onward = grad_copy(gfull.at[:, shard(owner)], owner, f_s.at[j - 1], partner)
-        onward.start()
-        forwards.append(onward)
-    grad_copy(go_h, partner, g_s.at[nz - 1], partner).wait_recv()
-    for j in range(1, nz):
-        owner = mate(j, 1 - core)
-        grad_copy(gfull.at[:, shard(owner)], owner, f_s.at[j - 1], partner).wait_recv()
     load_go.wait()
     load_wo.wait()
-
-    def d_piece(n, carry):
-        at = pl.ds(pl.multiple_of(n * half, half), half)
-        da[:, at] = dot_nt(gfull[...], wo[at, :]).astype(BF)
+    acc[...] = jnp.zeros_like(acc)
+
+    def use_shard(t):
+        grads = gfull[:, shard(t)]
+        acc[...] += dot_nt(grads, wo[:, shard(t)])
+        part = dot_tn(attn[...], grads).astype(BF)
+        for k in range(nctx // ntp):
+            i = t * (nctx // ntp) + k
+            there_y = lax.div(i, nx)
+            there_x = lax.rem(i, nx)
+            wos[0, there_x, there_y] = part[: cols // 2, k * strip : (k + 1) * strip]
+            wos[1, there_y, there_x] = part[cols // 2 :, k * strip : (k + 1) * strip]
+
+    def use_near(i, carry):
+        side = jnp.where(lax.rem(i, 2) == 0, core, 1 - core)
+        hop = jnp.where(i < 2, 0, jnp.where(i < 4, 1, nz - 1))
+        t = mate(hop, side)
+
+        @pl.when((i == 1) | (i == 3) | (i == 5))
+        def _():
+            grad_copy(gfull.at[:, shard(t)], t, f_s.at[0], partner).wait_recv()
+
+        use_shard(t)
         return carry
 
-    lax.fori_loop(0, 2, d_piece, 0)
+    lax.fori_loop(0, 6, use_near, 0)
+    for way in range(2):
+        relay_wait(way)
+    pass_shard(mate(2, core), 2)
+
+    def use_far(i, carry):
+        t = mate(2, jnp.where(i == 0, core, 1 - core))
+
+        @pl.when(i == 1)
+        def _():
+            grad_copy(gfull.at[:, shard(t)], t, f_s.at[2], partner).wait_recv()
+
+        use_shard(t)
+        return carry
+
+    lax.fori_loop(0, 2, use_far, 0)
+    da[...] = acc[...].astype(BF)
+    out_wos = pltpu.make_async_copy(wos, wos_o, st.at[4])
+    out_wos.start()
 
     dlk[...] = jnp.zeros_like(dlk)
     dlv[...] = jnp.zeros_like(dlv)
@@ -385,18 +456,6 @@
     lax.fori_loop(1, nctx, give, 0)
     dlr[ctx] = dls[ctx]
 
-    def out_weight(i, carry):
-        part = dot_tn(attn[...], gfull[:, strip_at(i)]).astype(BF)
-        there_y = lax.div(i, nx)
-        there_x = lax.rem(i, nx)
-        wos[0, there_x, there_y] = part[: cols // 2]
-        wos[1, there_y, there_x] = part[cols // 2 :]
-        return carry
-
-    lax.fori_loop(0, nctx, out_weight, 0)
-    out_wos = pltpu.make_async_copy(wos, wos_o, st.at[4])
-    out_wos.start()
-
     for j in range(1, nx):
         owner = lax.rem(x + j, nx)
         for i in range(ny):
@@ -435,7 +494,7 @@
     out_dk.start()
     out_dv = pltpu.make_async_copy(dvv, dv_o, st.at[3])
     out_dv.start()
-    for send in first_sends + forwards:
+    for send in first_sends + forwards + [relay(0), relay(1)]:
         send.wait_send()
     for copy in [out_attn, out_dq, out_dk, out_dv, out_wos] + own_strips:
         copy.wait()
@@ -515,6 +574,7 @@
             pltpu.VMEM((nctx, per, cols), BF),
             pltpu.VMEM((nctx, per, cols), BF),
             pltpu.VMEM((2, nx, ny, cols // 2, width // nctx), BF),
+            pltpu.VMEM((rows, cols), F32),
             dma((6,)),
             dma((5,)),
             dma((ntp // 2,)),
@@ -533,6 +593,8 @@
             dma((nx - 1,)),
             dma((ny - 1,)),
             dma((ny - 1,)),
+            dma((2,)),
+            dma((2,)),
         ],
         compiler_params=pltpu.CompilerParams(
             collective_id=1, has_side_effects=True, vmem_limit_bytes=64 * 1024 * 1024 - 65536

time: 128 us -> 126 us (0.984)
  Pallas kernels: 128 us -> 126 us
    pallas_call x1, Pallas kernels: 57.2 us -> 54.9 us  [attention_core(): pl.pallas_call(functools.partial(core_kernel, nctx, ntp, nx), out_shape=(...]
where the time goes in v5:
time: 126 us
  Pallas kernels  126 us (100%)
    pallas_call x1, Pallas kernels, gradients(): pl.pallas_call(functools.partial(grad_kernel, nctx, ntp, nx), out_shape=(...  68 us
    pallas_call x1, Pallas kernels, attention_core(): pl.pallas_call(functools.partial(core_kernel, nctx, ntp, nx), out_shape=(...  54.9 us
    pallas_call x1, Pallas kernels, settled(): pl.pallas_call(functools.partial(settle_kernel, count), out_shape=tuple((...  2.8 us

profile of v5, /device:TPU:1, one launch (start us, length us, event | category | flops | bytes accessed | tf_op | source)
XLA Modules:
  0.0 126.3 jit_solution(11876577543133202837)
XLA Ops:
  0.6 54.9 %attention_core.1 = (bf16[512,512]{1,0:T(8,128)(2,1)}, bf16[512,512]{1,0:T(8,128)(2,1)}, bf16[512,512]{1,0:T(8,128)(2,1)}, bf16[512,512]{1,0:T(8,128)(2,1)}, bf1...) custom-call(bf16[512,4096]{1,0:T(8,128)(2,1)} %tok_h.3, ...), custom_call_target="tpu_custom_call" | custom-call | tf_op jit(solution)/shard_map/attention_core/pallas_call | solution.py:542
  55.5 68.0 %gradients.1 = (bf16[512,512]{1,0:T(8,128)(2,1)}, bf16[512,512]{1,0:T(8,128)(2,1)}, f32[256,512]{1,0:T(8,128)}, f32[256,512]{1,0:T(8,128)}, f32[256,512]{1,0:T(8,128)}, /*index=5*/f32[512,256]{1,0:T(8,128)}) custom-call(bf16[512,512]{1,0:T(8,128)(2,1)} %get-tuple-element.19.dq_h, bf16[512,512]{1,0:T(8,128)(2,1)} %get-tuple-element.20.dk_h, ...), custom_call_target="tpu_custom_call" | custom-call | tf_op jit(solution)/shard_map/gradients/pallas_call | solution.py:1095
  123.5 2.8 %settled.1 = (bf16[512,512]{1,0:T(8,128)(2,1)}, bf16[512,512]{1,0:T(8,128)(2,1)}, f32[256,512]{1,0:T(8,128)}, f32[256,512]{1,0:T(8,128)}, f32[256,512]{1,0:T(8,128)}, /*index=5*/f32[512,256]{1,0:T(8,128)}) custom-call(bf16[512,512]{1,0:T(8,128)(2,1)} %get-tuple-element.26.refs_0_, bf16[512,512]{1,0:T(8,128)(2,1)} %get-tuple-element.27.refs_1_, ...), custom_call_target="tpu_custom_call" | custom-call | tf_op jit(solution)/shard_map/settled/pallas_call | solution.py:1197

commit v6 on v5

--- a/solution.py
+++ b/solution.py
@@ -35,6 +35,70 @@
 
 def one_hot(hit):
     return jnp.where(hit, 1.0, 0.0).astype(BF)
+
+
+def remote(source, target, send, recv, where):
+    return pltpu.make_async_remote_copy(
+        src_ref=source,
+        dst_ref=target,
+        send_sem=send,
+        recv_sem=recv,
+        device_id=where,
+        device_id_type=MESH,
+    )
+
+
+def summed_over_heads(ntp, chunk, p, q, zb, acc, p_s, p_r, z_s, z_r):
+    tp = lax.axis_index("tp")
+    nz = ntp // 2
+    core = lax.rem(tp, 2)
+    z = lax.div(tp, 2)
+    partner = {"tp": tp + 1 - 2 * core}
+
+    def first(i, carry):
+        p[i] = chunk(i * 2 + 1 - core).astype(BF)
+        remote(p.at[i], q.at[i], p_s.at[i], p_r.at[i], partner).start()
+        return carry
+
+    lax.fori_loop(0, nz, first, 0)
+
+    def second(j, carry):
+        i = lax.rem(z + j, nz)
+        part = chunk(i * 2 + core)
+        copy = remote(p.at[i], q.at[i], p_s.at[i], p_r.at[i], partner)
+        copy.wait_send()
+        copy.wait_recv()
+        part = part + q[i].astype(F32)
+
+        @pl.when(j < nz)
+        def _():
+            p[i] = part.astype(BF)
+            remote(
+                p.at[i], zb.at[z], z_s.at[j - 1], z_r.at[z], {"tp": i * 2 + core}
+            ).start()
+
+        @pl.when(j == nz)
+        def _():
+            acc[...] = part
+
+        return carry
+
+    lax.fori_loop(1, nz + 1, second, 0)
+
+
+def from_heads(ntp, p, zb, acc, z_s, z_r):
+    tp = lax.axis_index("tp")
+    nz = ntp // 2
+    core = lax.rem(tp, 2)
+    z = lax.div(tp, 2)
+    total = acc[...]
+    for j in range(1, nz):
+        i = lax.rem(z + j, nz)
+        copy = remote(p.at[i], zb.at[i], z_s.at[j - 1], z_r.at[i], {"tp": i * 2 + core})
+        copy.wait_send()
+        copy.wait_recv()
+        total = total + zb[i].astype(F32)
+    return total
 
 
 def core_kernel(
@@ -48,11 +112,13 @@
     wo_h,
     doc_ref,
     go_h,
-    attn_o,
+    out_o,
     dq_o,
     dk_o,
     dv_o,
     wos_o,
+    wfar_o,
+    wr_o,
     tx_o,
     ty_o,
     tok,
@@ -77,6 +143,11 @@
     dlr,
     wos,
     acc,
+    o_p,
+    o_q,
+    o_z,
+    o_a,
+    outv,
     ld,
     st,
     g_s,
@@ -97,6 +168,14 @@
     fy_r,
     h_s,
     h_r,
+    op_s,
+    op_r,
+    oz_s,
+    oz_r,
+    w0_s,
+    w0_r,
+    w1_s,
+    w1_r,
 ):
     ctx = lax.axis_index("ctx")
     ny = nctx // nx
@@ -162,6 +241,50 @@
     for send in first_sends:
         send.start()
 
+    strip = width // nctx
+    own_half = pl.ds(pl.multiple_of(core * (rows // 2), rows // 2), rows // 2)
+
+    def strip_at(i):
+        return pl.ds(pl.multiple_of(i * strip, strip), strip)
+
+    def x_copy(j, i, owner):
+        return pltpu.make_async_remote_copy(
+            src_ref=tok_h.at[own_half, strip_at(i * nx + lax.rem(x + j, nx))],
+            dst_ref=tx_o.at[owner, own_half, strip_at(i)],
+            send_sem=tx_s.at[j - 1, i],
+            recv_sem=tx_r.at[owner, i],
+            device_id={"ctx": y * nx + lax.rem(x + j, nx)},
+            device_id_type=MESH,
+        )
+
+    def y_copy(j, owner):
+        there = lax.rem(y + j, ny)
+        return pltpu.make_async_remote_copy(
+            src_ref=tok_h.at[own_half, pl.ds(pl.multiple_of(there * nx * strip, strip), nx * strip)],
+            dst_ref=ty_o.at[owner, own_half],
+            send_sem=ty_s.at[j - 1],
+            recv_sem=ty_r.at[owner],
+            device_id={"ctx": there * nx + x},
+            device_id_type=MESH,
+        )
+
+    def pass_on(ref, owner, send, recv):
+        return pltpu.make_async_remote_copy(
+            src_ref=ref.at[owner, own_half],
+            dst_ref=ref.at[owner, own_half],
+            send_sem=send,
+            recv_sem=recv,
+            device_id={"tp": partner},
+            device_id_type=MESH,
+        )
+
+    def send_tokens(j):
+        for i in range(ny):
+            x_copy(j, i, x).start()
+        y_copy(j, y).start()
+
+    send_tokens(1)
+    send_tokens(3)
     load_tok.wait()
 
     half = cols // 2
@@ -202,6 +325,7 @@
         return carry
 
     lax.fori_loop(0, 3, project, 0)
+    send_tokens(2)
 
     def land_wait(j, carry):
         source = lax.rem(ctx + j, nctx)
@@ -258,47 +382,6 @@
         relay(way).start()
         pass_shard(owner, way)
 
-    strip = width // nctx
-    own_half = pl.ds(pl.multiple_of(core * (rows // 2), rows // 2), rows // 2)
-
-    def strip_at(i):
-        return pl.ds(pl.multiple_of(i * strip, strip), strip)
-
-    def x_copy(j, i, owner):
-        return pltpu.make_async_remote_copy(
-            src_ref=tok.at[own_half, strip_at(i * nx + lax.rem(x + j, nx))],
-            dst_ref=tx_o.at[owner, own_half, strip_at(i)],
-            send_sem=tx_s.at[j - 1, i],
-            recv_sem=tx_r.at[owner, i],
-            device_id={"ctx": y * nx + lax.rem(x + j, nx)},
-            device_id_type=MESH,
-        )
-
-    def y_copy(j, owner):
-        there = lax.rem(y + j, ny)
-        return pltpu.make_async_remote_copy(
-            src_ref=tok.at[own_half, pl.ds(pl.multiple_of(there * nx * strip, strip), nx * strip)],
-            dst_ref=ty_o.at[owner, own_half],
-            send_sem=ty_s.at[j - 1],
-            recv_sem=ty_r.at[owner],
-            device_id={"ctx": there * nx + x},
-            device_id_type=MESH,
-        )
-
-    def pass_on(ref, owner, send, recv):
-        return pltpu.make_async_remote_copy(
-            src_ref=ref.at[owner, own_half],
-            dst_ref=ref.at[owner, own_half],
-            send_sem=send,
-            recv_sem=recv,
-            device_id={"tp": partner},
-            device_id_type=MESH,
-        )
-
-    for j in (1, 3, 2):
-        for i in range(ny):
-            x_copy(j, i, x).start()
-        y_copy(j, y).start()
     own_strips = [
         pltpu.make_async_copy(
             tok.at[:, strip_at(i * nx + x)], tx_o.at[x, :, strip_at(i)], t_l.at[i]
@@ -354,11 +437,13 @@
         return carry
 
     lax.fori_loop(0, rows // PAIR, forward, 0)
-    out_attn = pltpu.make_async_copy(attn, attn_o, st.at[0])
-    out_attn.start()
-
+    load_wo.wait()
+
+    def out_chunk(t):
+        return dot_nn(attn[...], wo[:, shard(t)])
+
+    summed_over_heads(ntp, out_chunk, o_p, o_q, o_z, o_a, op_s, op_r, oz_s, oz_r)
     load_go.wait()
-    load_wo.wait()
     acc[...] = jnp.zeros_like(acc)
 
     def use_shard(t):
@@ -403,6 +488,33 @@
     da[...] = acc[...].astype(BF)
     out_wos = pltpu.make_async_copy(wos, wos_o, st.at[4])
     out_wos.start()
+    rings = ((x, nx, lambda i: {"ctx": y * nx + i}), (y, ny, lambda i: {"ctx": i * nx + x}))
+    subs = (pl.ds(0, nx // 2), pl.ds(nx // 2, nx // 2))
+
+    def far_hop(side, way):
+        pos, n, at = rings[side]
+        return remote(
+            wos.at[side, lax.rem(pos + 2, n), subs[way]],
+            wfar_o.at[side, subs[way]],
+            w0_s.at[side, way],
+            w0_r.at[side, way],
+            at(lax.rem(pos + (1 if way == 0 else n - 1), n)),
+        )
+
+    def near_hop(side, way):
+        pos, n, at = rings[side]
+        there = lax.rem(pos + (1 if way == 0 else n - 1), n)
+        return remote(
+            wos.at[side, there, subs[1 - way]],
+            wr_o.at[side, way, subs[1 - way]],
+            w1_s.at[side, way],
+            w1_r.at[side, way],
+            at(there),
+        )
+
+    for way in range(2):
+        for side in range(2):
+            far_hop(side, way).start()
 
     dlk[...] = jnp.zeros_like(dlk)
     dlv[...] = jnp.zeros_like(dlv)
@@ -454,6 +566,9 @@
         return carry
 
     lax.fori_loop(1, nctx, give, 0)
+    for way in range(2):
+        for side in range(2):
+            near_hop(side, way).start()
     dlr[ctx] = dls[ctx]
 
     for j in range(1, nx):
@@ -494,9 +609,19 @@
     out_dk.start()
     out_dv = pltpu.make_async_copy(dvv, dv_o, st.at[3])
     out_dv.start()
+    outv[...] = (
+        tok[:, shard(tp)].astype(F32) + from_heads(ntp, o_p, o_z, o_a, oz_s, oz_r)
+    ).astype(BF)
+    out_out = pltpu.make_async_copy(outv, out_o, st.at[5])
+    out_out.start()
+    for way in range(2):
+        for side in range(2):
+            for copy in (far_hop(side, way), near_hop(side, way)):
+                copy.wait_send()
+                copy.wait_recv()
     for send in first_sends + forwards + [relay(0), relay(1)]:
         send.wait_send()
-    for copy in [out_attn, out_dq, out_dk, out_dv, out_wos] + own_strips:
+    for copy in [out_out, out_dq, out_dk, out_dv, out_wos] + own_strips:
         copy.wait()
     for j in range(1, nx):
         for i in range(ny):
@@ -547,11 +672,13 @@
             small,
             small,
             jax.ShapeDtypeStruct((2, nx, ny, cols // 2, width // nctx), BF),
+            jax.ShapeDtypeStruct((2, ny, cols // 2, width // nctx), BF),
+            jax.ShapeDtypeStruct((2, 2, ny, cols // 2, width // nctx), BF),
             jax.ShapeDtypeStruct((nx, rows, width // nx), BF),
             jax.ShapeDtypeStruct((ny, rows, width // ny), BF),
         ),
         in_specs=[hbm] * 5 + [pl.BlockSpec(memory_space=pltpu.VMEM), hbm],
-        out_specs=(hbm,) * 7,
+        out_specs=(hbm,) * 9,
         scratch_shapes=[
             pltpu.VMEM((rows, width), BF),
             pltpu.VMEM((3, width, cols), BF),
@@ -575,8 +702,13 @@
             pltpu.VMEM((nctx, per, cols), BF),
             pltpu.VMEM((2, nx, ny, cols // 2, width // nctx), BF),
             pltpu.VMEM((rows, cols), F32),
+            pltpu.VMEM((ntp // 2, rows, cols), BF),
+            pltpu.VMEM((ntp // 2, rows, cols), BF),
+            pltpu.VMEM((ntp // 2, rows, cols), BF),
+            pltpu.VMEM((rows, cols), F32),
+            pltpu.VMEM((rows, cols), BF),
             dma((6,)),
-            dma((5,)),
+            dma((6,)),
             dma((ntp // 2,)),
             dma((ntp,)),
             dma((ntp // 2,)),
@@ -595,6 +727,14 @@
             dma((ny - 1,)),
             dma((2,)),
             dma((2,)),
+            dma((ntp // 2,)),
+            dma((ntp // 2,)),
+            dma((ntp // 2 - 1,)),
+            dma((ntp // 2,)),
+            dma((2, 2)),
+            dma((2, 2)),
+            dma((2, 2)),
+            dma((2, 2)),
         ],
         compiler_params=pltpu.CompilerParams(
             collective_id=1, has_side_effects=True, vmem_limit_bytes=64 * 1024 * 1024 - 65536
@@ -610,36 +750,27 @@
     dq_h,
     dk_h,
     dv_h,
-    attn_h,
     wos_h,
+    wfar_h,
+    wr_h,
     tx_h,
     ty_h,
     wq_h,
     wk_h,
     wv_h,
-    wo_h,
-    tok_h,
     go_h,
-    out_o,
     gt_o,
     gq_o,
     gk_o,
     gv_o,
     gwo_o,
     w3,
-    wo,
     dcat,
-    attn,
-    rest,
     rest_g,
     gq,
     gk,
     gvx,
     gvy,
-    o_p,
-    o_q,
-    o_z,
-    o_a,
     d_p,
     d_q,
     d_z,
@@ -661,12 +792,9 @@
     wo_u,
     wo_a,
     ld,
+    dl,
     ag_s,
     ag_r,
-    op_s,
-    op_r,
-    oz_s,
-    oz_r,
     dp_s,
     dp_r,
     dz_s,
@@ -675,8 +803,6 @@
     rf_r,
     rs_s,
     rs_r,
-    w0_s,
-    w0_r,
     w1_s,
     w1_r,
     w2_s,
@@ -691,8 +817,8 @@
     core = lax.rem(tp, 2)
     z = lax.div(tp, 2)
     partner = tp + 1 - 2 * core
-    rows, cols = attn.shape
-    width = wo.shape[1]
+    rows, cols = rest_g.shape
+    width = w3.shape[0]
     strip = width // nctx
     gathered = nx * rows
     half = cols // 2
@@ -709,25 +835,11 @@
     def at_y(i):
         return {"ctx": i * nx + x}
 
-    def remote(source, target, send, recv, where):
-        return pltpu.make_async_remote_copy(
-            src_ref=source,
-            dst_ref=target,
-            send_sem=send,
-            recv_sem=recv,
-            device_id=where,
-            device_id_type=MESH,
-        )
-
-    loads = [
-        pltpu.make_async_copy(attn_h, attn, ld.at[0]),
-        pltpu.make_async_copy(wo_h, wo, ld.at[1]),
-    ]
+    loads = []
     for i, (d_h, w_h) in enumerate(((dq_h, wq_h), (dk_h, wk_h), (dv_h, wv_h))):
         lanes = pl.ds(i * cols, cols)
         loads.append(pltpu.make_async_copy(d_h, dcat.at[:, lanes], ld.at[2 + 2 * i]))
         loads.append(pltpu.make_async_copy(w_h, w3.at[:, lanes], ld.at[3 + 2 * i]))
-    loads.append(pltpu.make_async_copy(tok_h.at[:, block(tp)], rest, ld.at[8]))
     loads.append(pltpu.make_async_copy(go_h, rest_g, ld.at[9]))
     lo = pl.ds(0, half)
     hi = pl.ds(half, half)
@@ -750,6 +862,17 @@
                     ld.at[14 + 3 * side + min(k, 2)],
                 )
             )
+    loads.append(pltpu.make_async_copy(wfar_h, wo_far, ld.at[0]))
+    subs = (pl.ds(0, nx // 2), pl.ds(nx // 2, nx // 2))
+    for side in range(2):
+        for way in range(2):
+            loads.append(
+                pltpu.make_async_copy(
+                    wr_h.at[side, way, subs[1 - way]],
+                    wo_r.at[side, way, subs[1 - way]],
+                    dl.at[side, way],
+                )
+            )
     for load in loads:
         load.start()
 
@@ -815,89 +938,23 @@
         near_send(gather, 0).start()
         near_send(gather, 1).start()
 
-    subs = (pl.ds(0, nx // 2), pl.ds(nx // 2, nx // 2))
-
-    def far_hop(side, way):
+    def near_hop(side, way):
         pos, n, at = rings[side]
-        return remote(
-            wos_h.at[side, lax.rem(pos + 2, n), subs[way]],
-            wo_far.at[side, subs[way]],
-            w0_s.at[side, way],
-            w0_r.at[side, way],
-            at(lax.rem(pos + (1 if way == 0 else n - 1), n)),
-        )
-
-    def near_hop(side, way, added):
-        pos, n, at = rings[side]
-        part = subs[way if added else 1 - way]
+        part = subs[way]
         return remote(
             wo_nb.at[side, way, part],
             wo_r.at[side, way, part],
-            w1_s.at[side, way, 1 if added else 0],
-            w1_r.at[side, way, 1 if added else 0],
+            w1_s.at[side, way],
+            w1_r.at[side, way],
             at(lax.rem(pos + (1 if way == 0 else n - 1), n)),
         )
-
-    for way in range(2):
-        for side in range(2):
-            far_hop(side, way).start()
-
-    def out_chunk(t):
-        return dot_nn(attn[...], wo[:, block(t)])
 
     def tok_chunk(t):
         return dot_nt(dcat[...], w3[block(t), :])
 
-    def to_partner(i, chunk, p, q, p_s, p_r):
-        return remote(p.at[i], q.at[i], p_s.at[i], p_r.at[i], {"tp": partner})
-
-    def summed_over_heads(chunk, p, q, zb, acc, p_s, p_r, z_s, z_r):
-        def first(i, carry):
-            p[i] = chunk(i * 2 + 1 - core).astype(BF)
-            to_partner(i, chunk, p, q, p_s, p_r).start()
-            return carry
-
-        lax.fori_loop(0, nz, first, 0)
-
-        def second(j, carry):
-            i = lax.rem(z + j, nz)
-            part = chunk(i * 2 + core)
-            copy = to_partner(i, chunk, p, q, p_s, p_r)
-            copy.wait_send()
-            copy.wait_recv()
-            part = part + q[i].astype(F32)
-
-            @pl.when(j < nz)
-            def _():
-                p[i] = part.astype(BF)
-                remote(
-                    p.at[i], zb.at[z], z_s.at[j - 1], z_r.at[z], {"tp": i * 2 + core}
-                ).start()
-
-            @pl.when(j == nz)
-            def _():
-                acc[...] = part
-
-            return carry
-
-        lax.fori_loop(1, nz + 1, second, 0)
-
-    def from_heads(p, zb, acc, z_s, z_r):
-        total = acc[...]
-        for j in range(1, nz):
-            i = lax.rem(z + j, nz)
-            copy = remote(p.at[i], zb.at[i], z_s.at[j - 1], z_r.at[i], {"tp": i * 2 + core})
-            copy.wait_send()
-            copy.wait_recv()
-            total = total + zb[i].astype(F32)
-        return total
-
-    loads[0].wait()
-    loads[1].wait()
-    summed_over_heads(out_chunk, o_p, o_q, o_z, o_a, op_s, op_r, oz_s, oz_r)
-    for load in loads[2:8]:
+    for load in loads[:6]:
         load.wait()
-    summed_over_heads(tok_chunk, d_p, d_q, d_z, d_a, dp_s, dp_r, dz_s, dz_r)
+    summed_over_heads(ntp, tok_chunk, d_p, d_q, d_z, d_a, dp_s, dp_r, dz_s, dz_r)
     t_x = w3.at[pl.ds(0, gathered), pl.ds(0, width // nx)]
     t_y = w3.at[pl.ds(gathered, gathered), pl.ds(0, width // ny)]
     late = []
@@ -913,20 +970,15 @@
             near_recv(gather, step).wait_recv()
             relay(gather, step).start()
 
-    for load in loads[8:] + late:
+    for load in loads[6:] + late:
         load.wait()
-
     for side in range(2):
         for way in range(2):
-            near_hop(side, way, False).start()
-    for side in range(2):
-        for way in range(2):
-            far_hop(side, way).wait_recv()
             part = subs[way]
             wo_nb[side, way, part] = (
                 wo_nb[side, way, part].astype(F32) + wo_far[side, part].astype(F32)
             ).astype(BF)
-            near_hop(side, way, True).start()
+            near_hop(side, way).start()
 
     sends = (
         (gathers[0], 0, sq, rq, oq, y, at_y, 0),
@@ -1007,8 +1059,7 @@
             ).astype(BF)
             weight_near(item, way, True).start()
 
-    out_o[...] = (rest[...].astype(F32) + from_heads(o_p, o_z, o_a, oz_s, oz_r)).astype(BF)
-    gt_o[...] = (rest_g[...].astype(F32) + from_heads(d_p, d_z, d_a, dz_s, dz_r)).astype(BF)
+    gt_o[...] = (rest_g[...].astype(F32) + from_heads(ntp, d_p, d_z, d_a, dz_s, dz_r)).astype(BF)
 
     def second_hop(side, there, slot, owner):
         pos, n, at = ((y, ny, at_y), (x, nx, at_x))[side]
@@ -1023,11 +1074,9 @@
     for side in range(2):
         pos, m = ((y, ny), (x, nx))[side]
         for way in range(2):
-            far_hop(side, way).wait_send()
-            for added in (False, True):
-                copy = near_hop(side, way, added)
-                copy.wait_send()
-                copy.wait_recv()
+            copy = near_hop(side, way)
+            copy.wait_send()
+            copy.wait_recv()
 
         def add_up(j, carry):
             there = lax.rem(pos + j, m)
@@ -1073,9 +1122,10 @@
         gwo_o[pl.ds(side * half, half), :] = total
 
 
-def gradients(nctx, ntp, nx, core_out, tokens, w_query, w_key, w_value, w_out, grad_out):
-    attn, d_query, d_key, d_value, wos, tx, ty = core_out
-    rows, width = tokens.shape
+def gradients(nctx, ntp, nx, core_out, w_query, w_key, w_value, grad_out):
+    d_query, d_key, d_value, wos, wfar, wr, tx, ty = core_out
+    rows = grad_out.shape[0]
+    width = w_query.shape[0]
     cols = w_query.shape[1]
     ny = nctx // nx
     nz = ntp // 2
@@ -1096,26 +1146,21 @@
         functools.partial(grad_kernel, nctx, ntp, nx),
         out_shape=(
             small,
-            small,
             piece,
             piece,
             piece,
             jax.ShapeDtypeStruct((cols, strip), F32),
         ),
-        in_specs=[hbm] * 13,
-        out_specs=(vmem,) * 6,
+        in_specs=[hbm] * 12,
+        out_specs=(vmem,) * 5,
         scratch_shapes=[
             pltpu.VMEM((width, 3 * cols), BF),
-            pltpu.VMEM((cols, width), BF),
             pltpu.VMEM((rows, 3 * cols), BF),
-            pltpu.VMEM((rows, cols), BF),
-            pltpu.VMEM((rows, cols), BF),
             pltpu.VMEM((rows, cols), BF),
             pltpu.VMEM((nx, rows, cols), BF),
             pltpu.VMEM((ny, rows, cols), BF),
             pltpu.VMEM((nx, rows, half), BF),
             pltpu.VMEM((ny, rows, half), BF),
-            *heads_scratch,
             *heads_scratch,
             pltpu.VMEM((3, strip, cols), BF),
             pltpu.VMEM((3, strip, cols), BF),
@@ -1134,12 +1179,9 @@
             pltpu.VMEM((2, ny, half, strip), BF),
             pltpu.VMEM((cols, strip), F32),
             dma((20 + nx + ny,)),
+            dma((2, 2)),
             dma((4, 4)),
             dma((4, 4)),
-            dma((nz,)),
-            dma((nz,)),
-            dma((nz - 1,)),
-            dma((nz,)),
             dma((nz,)),
             dma((nz,)),
             dma((nz - 1,)),
@@ -1150,8 +1192,6 @@
             dma((4, 2, 2)),
             dma((2, 2)),
             dma((2, 2)),
-            dma((2, 2, 2)),
-            dma((2, 2, 2)),
             dma((2, nx - 1)),
             dma((2, nx)),
         ],
@@ -1163,15 +1203,14 @@
         d_query,
         d_key,
         d_value,
-        attn,
         wos,
+        wfar,
+        wr,
         tx,
         ty,
         w_query,
         w_key,
         w_value,
-        w_out,
-        tokens,
         grad_out,
     )
 
@@ -1206,12 +1245,11 @@
 
 
 def per_device(nctx, ntp, nx, tokens, w_query, w_key, w_value, w_out, block_doc, grad_out):
-    core_out = attention_core(
+    out, *core_out = attention_core(
         nctx, ntp, nx, tokens, w_query, w_key, w_value, w_out, block_doc, grad_out
     )
-    return settled(
-        gradients(nctx, ntp, nx, core_out, tokens, w_query, w_key, w_value, w_out, grad_out)
-    )
+    grads = gradients(nctx, ntp, nx, core_out, w_query, w_key, w_value, grad_out)
+    return settled((out, *grads))
 
 
 def solution(mesh):

time: 126 us -> 134 us (1.063)
  Pallas kernels: 126 us -> 134 us
    pallas_call x1, Pallas kernels: 54.9 us -> 65.7 us  [attention_core(): pl.pallas_call(functools.partial(core_kernel, nctx, ntp, nx), out_shape=(...]
    pallas_call x1, Pallas kernels: 68 us -> 65.2 us  [gradients(): pl.pallas_call(functools.partial(grad_kernel, nctx, ntp, nx), out_shape=(...]
where the time goes in v6:
time: 134 us
  Pallas kernels  134 us (100%)
    pallas_call x1, Pallas kernels, attention_core(): pl.pallas_call(functools.partial(core_kernel, nctx, ntp, nx), out_shape=(...  65.7 us
    pallas_call x1, Pallas kernels, gradients(): pl.pallas_call(functools.partial(grad_kernel, nctx, ntp, nx), out_shape=(...  65.2 us
    pallas_call x1, Pallas kernels, settled(): pl.pallas_call(functools.partial(settle_kernel, count), out_shape=tuple((...  2.8 us

profile of v6, /device:TPU:1, one launch (start us, length us, event | category | flops | bytes accessed | tf_op | source)
XLA Modules:
  0.0 134.3 jit_solution(1050465556390536160)
XLA Ops:
  0.6 65.7 %attention_core.1 = (bf16[512,512]{1,0:T(8,128)(2,1)}, bf16[512,512]{1,0:T(8,128)(2,1)}, bf16[512,512]{1,0:T(8,128)(2,1)}, bf16[512,512]{1,0:T(8,128)(2,1)}, bf1...) custom-call(bf16[512,4096]{1,0:T(8,128)(2,1)} %tok_h.1, ...), custom_call_target="tpu_custom_call" | custom-call | tf_op jit(solution)/shard_map/attention_core/pallas_call | solution.py:667
  66.3 65.2 %gradients.1 = (bf16[512,512]{1,0:T(8,128)(2,1)}, f32[256,512]{1,0:T(8,128)}, f32[256,512]{1,0:T(8,128)}, f32[256,512]{1,0:T(8,128)}, f32[512,256]{1,0:T(8,128)}) custom-call(bf16[512,512]{1,0:T(8,128)(2,1)} %get-tuple-element.21.dq_h, bf16[512,512]{1,0:T(8,128)(2,1)} %get-tuple-element.22.dk_h, bf16[512,512]{1,0:T(8,128)(2,1)} %get-tuple-element.23.dv_h, ...), custom_call_target="tpu_custom_call" | custom-call | tf_op jit(solution)/shard_map/gradients/pallas_call | solution.py:1145
  131.5 2.8 %settled.1 = (bf16[512,512]{1,0:T(8,128)(2,1)}, bf16[512,512]{1,0:T(8,128)(2,1)}, f32[256,512]{1,0:T(8,128)}, f32[256,512]{1,0:T(8,128)}, f32[256,512]{1,0:T(8,128)}, /*index=5*/f32[512,256]{1,0:T(8,128)}) custom-call(bf16[512,512]{1,0:T(8,128)(2,1)} %get-tuple-element.20.refs_0_, bf16[512,512]{1,0:T(8,128)(2,1)} %get-tuple-element.29.refs_1_, ...), custom_call_target="tpu_custom_call" | custom-call | tf_op jit(solution)/shard_map/settled/pallas_call | solution.py:1236

commit v7 on v6

--- a/solution.py
+++ b/solution.py
@@ -249,7 +249,7 @@
 
     def x_copy(j, i, owner):
         return pltpu.make_async_remote_copy(
-            src_ref=tok_h.at[own_half, strip_at(i * nx + lax.rem(x + j, nx))],
+            src_ref=tok.at[own_half, strip_at(i * nx + lax.rem(x + j, nx))],
             dst_ref=tx_o.at[owner, own_half, strip_at(i)],
             send_sem=tx_s.at[j - 1, i],
             recv_sem=tx_r.at[owner, i],
@@ -260,7 +260,7 @@
     def y_copy(j, owner):
         there = lax.rem(y + j, ny)
         return pltpu.make_async_remote_copy(
-            src_ref=tok_h.at[own_half, pl.ds(pl.multiple_of(there * nx * strip, strip), nx * strip)],
+            src_ref=tok.at[own_half, pl.ds(pl.multiple_of(there * nx * strip, strip), nx * strip)],
             dst_ref=ty_o.at[owner, own_half],
             send_sem=ty_s.at[j - 1],
             recv_sem=ty_r.at[owner],
@@ -283,8 +283,6 @@
             x_copy(j, i, x).start()
         y_copy(j, y).start()
 
-    send_tokens(1)
-    send_tokens(3)
     load_tok.wait()
 
     half = cols // 2
@@ -325,7 +323,6 @@
         return carry
 
     lax.fori_loop(0, 3, project, 0)
-    send_tokens(2)
 
     def land_wait(j, carry):
         source = lax.rem(ctx + j, nctx)
@@ -368,7 +365,9 @@
         ).wait_recv()
 
     lax.fori_loop(1, nctx, land_wait, 0)
-
+    send_tokens(1)
+    send_tokens(3)
+    send_tokens(2)
     forwards = []
 
     def pass_shard(owner, slot):
@@ -381,6 +380,7 @@
         grad_copy(gfull.at[:, shard(owner)], owner, f_s.at[way], partner).wait_recv()
         relay(way).start()
         pass_shard(owner, way)
+
 
     own_strips = [
         pltpu.make_async_copy(
@@ -444,47 +444,44 @@
 
     summed_over_heads(ntp, out_chunk, o_p, o_q, o_z, o_a, op_s, op_r, oz_s, oz_r)
     load_go.wait()
-    acc[...] = jnp.zeros_like(acc)
-
-    def use_shard(t):
-        grads = gfull[:, shard(t)]
-        acc[...] += dot_nt(grads, wo[:, shard(t)])
+
+    def use_chip(hop, fresh):
+        chip = lax.rem(z + hop, nz)
+        both = pl.ds(pl.multiple_of(chip * 2 * cols, 2 * cols), 2 * cols)
+        grads = gfull[:, both]
+        product = dot_nt(grads, wo[:, both])
+        if fresh:
+            acc[...] = product
+        else:
+            acc[...] += product
         part = dot_tn(attn[...], grads).astype(BF)
-        for k in range(nctx // ntp):
-            i = t * (nctx // ntp) + k
+        each = 2 * (nctx // ntp)
+        for k in range(each):
+            i = chip * each + k
             there_y = lax.div(i, nx)
             there_x = lax.rem(i, nx)
             wos[0, there_x, there_y] = part[: cols // 2, k * strip : (k + 1) * strip]
             wos[1, there_y, there_x] = part[cols // 2 :, k * strip : (k + 1) * strip]
 
+    def other_core(hop, slot):
+        t = mate(hop, 1 - core)
+        grad_copy(gfull.at[:, shard(t)], t, f_s.at[slot], partner).wait_recv()
+
+    other_core(0, 0)
+    use_chip(0, True)
+
     def use_near(i, carry):
-        side = jnp.where(lax.rem(i, 2) == 0, core, 1 - core)
-        hop = jnp.where(i < 2, 0, jnp.where(i < 4, 1, nz - 1))
-        t = mate(hop, side)
-
-        @pl.when((i == 1) | (i == 3) | (i == 5))
-        def _():
-            grad_copy(gfull.at[:, shard(t)], t, f_s.at[0], partner).wait_recv()
-
-        use_shard(t)
+        hop = 1 + (nz - 2) * i
+        other_core(hop, 0)
+        use_chip(hop, False)
         return carry
 
-    lax.fori_loop(0, 6, use_near, 0)
+    lax.fori_loop(0, 2, use_near, 0)
     for way in range(2):
         relay_wait(way)
     pass_shard(mate(2, core), 2)
-
-    def use_far(i, carry):
-        t = mate(2, jnp.where(i == 0, core, 1 - core))
-
-        @pl.when(i == 1)
-        def _():
-            grad_copy(gfull.at[:, shard(t)], t, f_s.at[2], partner).wait_recv()
-
-        use_shard(t)
-        return carry
-
-    lax.fori_loop(0, 2, use_far, 0)
+    other_core(2, 2)
+    use_chip(2, False)
     da[...] = acc[...].astype(BF)
     out_wos = pltpu.make_async_copy(wos, wos_o, st.at[4])
     out_wos.start()

time: 134 us -> 120 us (0.90)
  Pallas kernels: 134 us -> 120 us
    pallas_call x1, Pallas kernels: 65.2 us -> 57.3 us  [gradients(): pl.pallas_call(functools.partial(grad_kernel, nctx, ntp, nx), out_shape=(...]
    pallas_call x1, Pallas kernels: 65.7 us -> 59.5 us  [attention_core(): pl.pallas_call(functools.partial(core_kernel, nctx, ntp, nx), out_shape=(...]
where the time goes in v7:
time: 120 us
  Pallas kernels  120 us (100%)
    pallas_call x1, Pallas kernels, attention_core(): pl.pallas_call(functools.partial(core_kernel, nctx, ntp, nx), out_shape=(...  59.5 us
    pallas_call x1, Pallas kernels, gradients(): pl.pallas_call(functools.partial(grad_kernel, nctx, ntp, nx), out_shape=(...  57.3 us
    pallas_call x1, Pallas kernels, settled(): pl.pallas_call(functools.partial(settle_kernel, count), out_shape=tuple((...  2.8 us

profile of v7, /device:TPU:1, one launch (start us, length us, event | category | flops | bytes accessed | tf_op | source)
XLA Modules:
  0.0 120.2 jit_solution(12583532384466236743)
XLA Ops:
  0.6 59.5 %attention_core.1 = (bf16[512,512]{1,0:T(8,128)(2,1)}, bf16[512,512]{1,0:T(8,128)(2,1)}, bf16[512,512]{1,0:T(8,128)(2,1)}, bf16[512,512]{1,0:T(8,128)(2,1)}, bf1...) custom-call(bf16[512,4096]{1,0:T(8,128)(2,1)} %tok_h.1, ...), custom_call_target="tpu_custom_call" | custom-call | tf_op jit(solution)/shard_map/attention_core/pallas_call | solution.py:664
  60.1 57.3 %gradients.1 = (bf16[512,512]{1,0:T(8,128)(2,1)}, f32[256,512]{1,0:T(8,128)}, f32[256,512]{1,0:T(8,128)}, f32[256,512]{1,0:T(8,128)}, f32[512,256]{1,0:T(8,128)}) custom-call(bf16[512,512]{1,0:T(8,128)(2,1)} %get-tuple-element.21.dq_h, bf16[512,512]{1,0:T(8,128)(2,1)} %get-tuple-element.22.dk_h, bf16[512,512]{1,0:T(8,128)(2,1)} %get-tuple-element.23.dv_h, ...), custom_call_target="tpu_custom_call" | custom-call | tf_op jit(solution)/shard_map/gradients/pallas_call | solution.py:1142
  117.4 2.8 %settled.1 = (bf16[512,512]{1,0:T(8,128)(2,1)}, bf16[512,512]{1,0:T(8,128)(2,1)}, f32[256,512]{1,0:T(8,128)}, f32[256,512]{1,0:T(8,128)}, f32[256,512]{1,0:T(8,128)}, /*index=5*/f32[512,256]{1,0:T(8,128)}) custom-call(bf16[512,512]{1,0:T(8,128)(2,1)} %get-tuple-element.20.refs_0_, bf16[512,512]{1,0:T(8,128)(2,1)} %get-tuple-element.29.refs_1_, ...), custom_call_target="tpu_custom_call" | custom-call | tf_op jit(solution)/shard_map/settled/pallas_call | solution.py:1233

commit v8 on v7

--- a/solution.py
+++ b/solution.py
@@ -200,6 +200,19 @@
     def mate(j, side):
         return lax.rem(z + j, nz) * 2 + side
 
+    barrier = pltpu.get_barrier_semaphore()
+
+    def greet(i, carry):
+        pl.semaphore_signal(
+            barrier, inc=1, device_id={"ctx": lax.rem(ctx + i, nctx)}, device_id_type=MESH
+        )
+        return carry
+
+    lax.fori_loop(1, nctx, greet, 0)
+    pl.semaphore_signal(barrier, inc=1, device_id={"tp": partner}, device_id_type=MESH)
+    for j in range(1, nz):
+        pl.semaphore_signal(barrier, inc=1, device_id={"tp": mate(j, core)}, device_id_type=MESH)
+
     load_tok = pltpu.make_async_copy(tok_h, tok, ld.at[0])
     load_tok.start()
     for i, w_h in enumerate((wk_h, wv_h, wq_h)):
@@ -209,18 +222,6 @@
     load_go = pltpu.make_async_copy(go_h, gfull.at[:, shard(tp)], ld.at[5])
     load_go.start()
 
-    barrier = pltpu.get_barrier_semaphore()
-
-    def greet(i, carry):
-        pl.semaphore_signal(
-            barrier, inc=1, device_id={"ctx": lax.rem(ctx + i, nctx)}, device_id_type=MESH
-        )
-        return carry
-
-    lax.fori_loop(1, nctx, greet, 0)
-    pl.semaphore_signal(barrier, inc=1, device_id={"tp": partner}, device_id_type=MESH)
-    for j in range(1, nz):
-        pl.semaphore_signal(barrier, inc=1, device_id={"tp": mate(j, core)}, device_id_type=MESH)
     pl.semaphore_wait(barrier, nctx - 1 + nz)
 
     def grad_copy(source, owner, send, target):
@@ -832,6 +833,24 @@
     def at_y(i):
         return {"ctx": i * nx + x}
 
+    barrier = pltpu.get_barrier_semaphore()
+    for j in range(1, nx):
+        pl.semaphore_signal(
+            barrier, inc=1, device_id=at_x(lax.rem(x + j, nx)), device_id_type=MESH
+        )
+    for j in range(1, ny):
+        pl.semaphore_signal(
+            barrier, inc=1, device_id=at_y(lax.rem(y + j, ny)), device_id_type=MESH
+        )
+    for j in range(1, nz):
+        pl.semaphore_signal(
+            barrier,
+            inc=1,
+            device_id={"tp": lax.rem(z + j, nz) * 2 + core},
+            device_id_type=MESH,
+        )
+    pl.semaphore_signal(barrier, inc=1, device_id={"tp": partner}, device_id_type=MESH)
+
     loads = []
     for i, (d_h, w_h) in enumerate(((dq_h, wq_h), (dk_h, wk_h), (dv_h, wv_h))):
         lanes = pl.ds(i * cols, cols)
@@ -873,23 +892,6 @@
     for load in loads:
         load.start()
 
-    barrier = pltpu.get_barrier_semaphore()
-    for j in range(1, nx):
-        pl.semaphore_signal(
-            barrier, inc=1, device_id=at_x(lax.rem(x + j, nx)), device_id_type=MESH
-        )
-    for j in range(1, ny):
-        pl.semaphore_signal(
-            barrier, inc=1, device_id=at_y(lax.rem(y + j, ny)), device_id_type=MESH
-        )
-    for j in range(1, nz):
-        pl.semaphore_signal(
-            barrier,
-            inc=1,
-            device_id={"tp": lax.rem(z + j, nz) * 2 + core},
-            device_id_type=MESH,
-        )
-    pl.semaphore_signal(barrier, inc=1, device_id={"tp": partner}, device_id_type=MESH)
     pl.semaphore_wait(barrier, nx + ny + nz - 2)
 
     def near_send(gather, step):

time: 120 us -> 120 us (level)
  no operation moved by 1% of the time
where the time goes in v8:
time: 120 us
  Pallas kernels  120 us (100%)
    pallas_call x1, Pallas kernels, attention_core(): pl.pallas_call(functools.partial(core_kernel, nctx, ntp, nx), out_shape=(...  59.5 us
    pallas_call x1, Pallas kernels, gradients(): pl.pallas_call(functools.partial(grad_kernel, nctx, ntp, nx), out_shape=(...  57.2 us
    pallas_call x1, Pallas kernels, settled(): pl.pallas_call(functools.partial(settle_kernel, count), out_shape=tuple((...  2.8 us

profile of v8, /device:TPU:1, one launch (start us, length us, event | category | flops | bytes accessed | tf_op | source)
XLA Modules:
  0.0 120.2 jit_solution(15743885051938274570)
XLA Ops:
  0.6 59.5 %attention_core.1 = (bf16[512,512]{1,0:T(8,128)(2,1)}, bf16[512,512]{1,0:T(8,128)(2,1)}, bf16[512,512]{1,0:T(8,128)(2,1)}, bf16[512,512]{1,0:T(8,128)(2,1)}, bf1...) custom-call(bf16[512,4096]{1,0:T(8,128)(2,1)} %tok_h.1, ...), custom_call_target="tpu_custom_call" | custom-call | tf_op jit(solution)/shard_map/attention_core/pallas_call | solution.py:665
  60.1 57.2 %gradients.1 = (bf16[512,512]{1,0:T(8,128)(2,1)}, f32[256,512]{1,0:T(8,128)}, f32[256,512]{1,0:T(8,128)}, f32[256,512]{1,0:T(8,128)}, f32[512,256]{1,0:T(8,128)}) custom-call(bf16[512,512]{1,0:T(8,128)(2,1)} %get-tuple-element.21.dq_h, bf16[512,512]{1,0:T(8,128)(2,1)} %get-tuple-element.22.dk_h, bf16[512,512]{1,0:T(8,128)(2,1)} %get-tuple-element.23.dv_h, ...), custom_call_target="tpu_custom_call" | custom-call | tf_op jit(solution)/shard_map/gradients/pallas_call | solution.py:1144
  117.4 2.8 %settled.1 = (bf16[512,512]{1,0:T(8,128)(2,1)}, bf16[512,512]{1,0:T(8,128)(2,1)}, f32[256,512]{1,0:T(8,128)}, f32[256,512]{1,0:T(8,128)}, f32[256,512]{1,0:T(8,128)}, /*index=5*/f32[512,256]{1,0:T(8,128)}) custom-call(bf16[512,512]{1,0:T(8,128)(2,1)} %get-tuple-element.20.refs_0_, bf16[512,512]{1,0:T(8,128)(2,1)} %get-tuple-element.29.refs_1_, ...), custom_call_target="tpu_custom_call" | custom-call | tf_op jit(solution)/shard_map/settled/pallas_call | solution.py:1235
